TPU v7x, 16 devices: a whole 2x2x2 slice. The times are simulated.
16 devices in a mesh: gp: 16 (over z, y, x, core).
Axes of the slice: x: 2, y: 2, z: 2, core: 2. Of those that a mesh axis runs over, the one named last changes fastest.
Arguments:
- grid_in: bfloat16 [16384, 164], P('gp')
- mesh_static: bfloat16 [8192, 3], P('gp')
- edge_static: bfloat16 [24576, 4], P('gp')
- send_rows: int32 [256, 64], P('gp')
- edge_src: int32 [24576], P('gp')
- edge_dst: int32 [24576], P('gp')
- w_grid_in: bfloat16 [164, 256], replicated
- w_mesh_in: bfloat16 [3, 256], replicated
- w_edge_in: bfloat16 [4, 256], replicated
- w_edge_up: bfloat16 [768, 256], replicated
- w_mesh_up: bfloat16 [512, 256], replicated
- w_grid_up: bfloat16 [256, 256], replicated
- w_second: bfloat16 [6, 256, 256], replicated
- vectors: float32 [6, 4, 256], replicated
- d_mesh_out: bfloat16 [8192, 256], P('gp')
- d_grid_out: bfloat16 [16384, 256], P('gp')
Outputs:
- output 1: bfloat16 [8192, 256], P('gp')
- output 2: bfloat16 [16384, 256], P('gp')
- output 3: float32 [16384, 164], P('gp')
- output 4: float32 [164, 256], replicated
- output 5: float32 [3, 256], replicated
- output 6: float32 [4, 256], replicated
- output 7: float32 [768, 256], replicated
- output 8: float32 [512, 256], replicated
- output 9: float32 [256, 256], replicated
- output 10: float32 [6, 256, 256], replicated
- output 11: float32 [6, 4, 256], replicated
All inputs are finite; a program needn't handle non-finite values.
Results may differ from a plain program's by a relative error of at most 0.02.
Values are sent between devices in bfloat16 or wider.
A program may use at most 1 GiB of HBM per device.

v0:
```python
import jax
import jax.numpy as jnp
from jax import lax
from jax.sharding import PartitionSpec as P

LN_EPS = 1e-5
AXIS_NAME = 'gp'


def matmul(lhs, rhs):
    return jnp.dot(lhs, rhs, preferred_element_type=jnp.float32)


def contract_rows(lhs, rhs):
    return lax.dot_general(lhs, rhs, (((0,), (0,)), ((), ())), preferred_element_type=jnp.float32)


def contract_cols(lhs, rhs):
    return lax.dot_general(lhs, rhs, (((1,), (1,)), ((), ())), preferred_element_type=jnp.float32)


def mlp_tail(pre_act, w_two, vec_rows):
    pre_bias = pre_act + vec_rows[0]
    hidden = jax.nn.silu(pre_bias).astype(jnp.bfloat16)
    out_lin = matmul(hidden, w_two) + vec_rows[1]
    centered = out_lin - jnp.mean(out_lin, axis=-1, keepdims=True)
    inv_std = lax.rsqrt(jnp.mean(centered * centered, axis=-1, keepdims=True) + LN_EPS)
    normed = centered * inv_std
    return normed * vec_rows[2] + vec_rows[3], (pre_bias, hidden, normed, inv_std)


def mlp_tail_back(saved, w_two, vec_rows, d_out):
    pre_bias, hidden, normed, inv_std = saved
    d_normed = d_out * vec_rows[2]
    d_lin = inv_std * (d_normed - jnp.mean(d_normed, axis=-1, keepdims=True) - normed * jnp.mean(d_normed * normed, axis=-1, keepdims=True))
    d_lin_bf = d_lin.astype(jnp.bfloat16)
    d_w_two = contract_rows(hidden, d_lin_bf)
    d_hidden = contract_cols(d_lin_bf, w_two)
    sig_pre = jax.nn.sigmoid(pre_bias)
    d_pre = d_hidden * sig_pre * (1.0 + pre_bias * (1.0 - sig_pre))
    d_vec = jnp.stack([jnp.sum(d_pre, axis=0), jnp.sum(d_lin, axis=0), jnp.sum(d_out * normed, axis=0), jnp.sum(d_out, axis=0)])
    return d_pre.astype(jnp.bfloat16), d_w_two, d_vec


def solution(mesh):
    row_spec = P(AXIS_NAME, None)
    edge_spec = P(AXIS_NAME)
    rep_spec = P()
    in_specs = (row_spec, row_spec, row_spec, row_spec, edge_spec, edge_spec) + (rep_spec,) * 8 + (row_spec, row_spec)
    out_specs = (row_spec, row_spec, row_spec) + (rep_spec,) * 8

    def local_step(grid_in, mesh_static, edge_static, send_rows, edge_src, edge_dst, w_grid_in, w_mesh_in, w_edge_in, w_edge_up, w_mesh_up, w_grid_up, w_second, vectors, d_mesh_out, d_grid_out):
        latent = w_grid_up.shape[0]
        grid_rows = grid_in.shape[0]
        mesh_rows = mesh_static.shape[0]
        slot_rows = send_rows.size
        send_flat = send_rows.reshape(-1)
        up_edge = w_edge_up[:latent]
        up_send = w_edge_up[latent:2 * latent]
        up_recv = w_edge_up[2 * latent:]
        node_self = w_mesh_up[:latent]
        node_agg = w_mesh_up[latent:]

        grid_emb, grid_save = mlp_tail(matmul(grid_in, w_grid_in), w_second[0], vectors[0])
        grid_lat = grid_emb.astype(jnp.bfloat16)
        mesh_emb, mesh_save = mlp_tail(matmul(mesh_static, w_mesh_in), w_second[1], vectors[1])
        mesh_lat = mesh_emb.astype(jnp.bfloat16)
        edge_emb, edge_save = mlp_tail(matmul(edge_static, w_edge_in), w_second[2], vectors[2])
        edge_lat = edge_emb.astype(jnp.bfloat16)

        outgoing = jnp.take(grid_lat, send_flat, axis=0)
        incoming = lax.all_to_all(outgoing, AXIS_NAME, 0, 0, tiled=True)

        edge_pre = (matmul(edge_lat, up_edge)
                    + jnp.take(matmul(incoming, up_send), edge_src, axis=0)
                    + jnp.take(matmul(mesh_lat, up_recv), edge_dst, axis=0))
        edge_upd, upd_save = mlp_tail(edge_pre, w_second[3], vectors[3])
        edge_new = (edge_lat.astype(jnp.float32) + edge_upd).astype(jnp.bfloat16)
        agg_sum = jax.ops.segment_sum(edge_new.astype(jnp.float32), edge_dst, num_segments=mesh_rows).astype(jnp.bfloat16)
        node_upd, node_save = mlp_tail(matmul(mesh_lat, node_self) + matmul(agg_sum, node_agg), w_second[4], vectors[4])
        mesh_out = (mesh_lat.astype(jnp.float32) + node_upd).astype(jnp.bfloat16)
        cell_upd, cell_save = mlp_tail(matmul(grid_lat, w_grid_up), w_second[5], vectors[5])
        grid_out = (grid_lat.astype(jnp.float32) + cell_upd).astype(jnp.bfloat16)

        d_grid_top = d_grid_out.astype(jnp.float32)
        d_mesh_top = d_mesh_out.astype(jnp.float32)
        d_pre5, d_two5, d_vec5 = mlp_tail_back(cell_save, w_second[5], vectors[5], d_grid_top)
        d_w_grid_up = contract_rows(grid_lat, d_pre5)
        d_grid_lat = d_grid_top + contract_cols(d_pre5, w_grid_up)
        d_pre4, d_two4, d_vec4 = mlp_tail_back(node_save, w_second[4], vectors[4], d_mesh_top)
        d_w_mesh_up = jnp.concatenate([contract_rows(mesh_lat, d_pre4), contract_rows(agg_sum, d_pre4)], axis=0)
        d_mesh_lat = d_mesh_top + contract_cols(d_pre4, node_self)
        d_agg = contract_cols(d_pre4, node_agg)
        d_edge_new = jnp.take(d_agg, edge_dst, axis=0)
        d_pre3, d_two3, d_vec3 = mlp_tail_back(upd_save, w_second[3], vectors[3], d_edge_new)
        d_pre3_wide = d_pre3.astype(jnp.float32)
        d_slot_pre = jax.ops.segment_sum(d_pre3_wide, edge_src, num_segments=slot_rows).astype(jnp.bfloat16)
        d_node_pre = jax.ops.segment_sum(d_pre3_wide, edge_dst, num_segments=mesh_rows).astype(jnp.bfloat16)
        d_w_edge_up = jnp.concatenate([contract_rows(edge_lat, d_pre3), contract_rows(incoming, d_slot_pre), contract_rows(mesh_lat, d_node_pre)], axis=0)
        d_edge_lat = d_edge_new + contract_cols(d_pre3, up_edge)
        d_mesh_lat = d_mesh_lat + contract_cols(d_node_pre, up_recv)
        d_incoming = contract_cols(d_slot_pre, up_send).astype(jnp.bfloat16)
        d_outgoing = lax.all_to_all(d_incoming, AXIS_NAME, 0, 0, tiled=True)
        d_grid_lat = d_grid_lat + jax.ops.segment_sum(d_outgoing.astype(jnp.float32), send_flat, num_segments=grid_rows)
        d_pre2, d_two2, d_vec2 = mlp_tail_back(edge_save, w_second[2], vectors[2], d_edge_lat)
        d_w_edge_in = contract_rows(edge_static, d_pre2)
        d_pre1, d_two1, d_vec1 = mlp_tail_back(mesh_save, w_second[1], vectors[1], d_mesh_lat)
        d_w_mesh_in = contract_rows(mesh_static, d_pre1)
        d_pre0, d_two0, d_vec0 = mlp_tail_back(grid_save, w_second[0], vectors[0], d_grid_lat)
        d_w_grid_in = contract_rows(grid_in, d_pre0)
        d_grid_in = contract_cols(d_pre0, w_grid_in)

        weight_grads = (d_w_grid_in, d_w_mesh_in, d_w_edge_in, d_w_edge_up, d_w_mesh_up, d_w_grid_up,
                        jnp.stack([d_two0, d_two1, d_two2, d_two3, d_two4, d_two5]),
                        jnp.stack([d_vec0, d_vec1, d_vec2, d_vec3, d_vec4, d_vec5]))
        weight_grads = lax.psum(weight_grads, AXIS_NAME)
        return (mesh_out, grid_out, d_grid_in) + weight_grads

    return jax.shard_map(local_step, mesh=mesh, in_specs=in_specs, out_specs=out_specs, check_vma=False)
```

profile of v0, /device:TPU:0, one launch (start us, length us, event | category | flops | bytes accessed | tf_op | source)
XLA Modules:
  0.0 260.7 jit_solution(5031395038859406310)
XLA Ops:
  13.8 3.9 %gather_fusion = bf16[1024,256]{1,0:T(8,128)(2,1)S(1)} fusion(bf16[1024,256]{1,0:T(8,128)(2,1)S(1)} %copy.38, s32[1024]{0:T(1024)S(1)} %broadcast_clamp_fusion), kind=kCustom, calls=%fused_computation.2 | custom fusion | bytes 1052672 | tf_op jit(solution)/shard_map/jit(_take)/gather | solution.py:71
  18.8 5.9 %all-to-all-start = ((bf16[16,64,256]{2,1,0:T(8,128)(2,1)}), bf16[16,64,256]{2,1,0:T(8,128)(2,1)}, u32[]{:S(2)}, u32[]{:S(2)}) async-start(bf16[16,64,256]{2,1,0:T(8,128)(2,1)} %broadcast_select_fusion), calls=%async_computation | async-start | bytes 1048576 | tf_op jit(solution)/shard_map/all_to_all | solution.py:72
  32.3 2.3 fusion.130
  42.2 2.2 fusion.111
  44.4 2.1 copy.51
  48.3 1.8 fusion.122
  50.8 4.6 %gather_fusion.2 = f32[1536,256]{1,0:T(8,128)} fusion(f32[512,256]{1,0:T(8,128)S(1)} %fusion.91, s32[2048]{0:T(1024)S(1)} %get-tuple-element.129), kind=kCustom, calls=%fused_computation.clone | custom fusion | bytes 3151872 | tf_op jit(solution)/shard_map/jit(_take)/gather | solution.py:76
  58.0 4.7 %gather_fusion.1 = f32[1536,256]{1,0:T(8,128)} fusion(f32[1024,256]{1,0:T(8,128)S(1)} %fusion.94, s32[2048]{0:T(1024)S(1)} %get-tuple-element.130), kind=kCustom, calls=%fused_computation.3 | custom fusion | bytes 3151872 | tf_op jit(solution)/shard_map/jit(_take)/gather | solution.py:75
  62.7 2.8 %fusion.3 = f32[1536,256]{1,0:T(8,128)S(1)} fusion(bf16[1536,256]{0,1:T(8,128)(2,1)} %add_convert_fusion.1, f32[1536,256]{1,0:T(8,128)} %gather_fusion.2, f32[1536,256]{1,0:T(8,128)} %gather_fusion.1, f32[256]{0:T(256)S(1)} %bitcast.260, pred[1536]{0:T(1024)(128)(4,1)S(1)} %get-tuple-element.131, pred[1536]{0:T(1024)(128)(4,1)S(1)} %copy-done.100, ...), kind=kOutput, calls=%fused_computation.16 | convolution fusion | flops 203292672 | bytes 5641216 | tf_op jit(solution)/shard_map/dot_general | solution.py:11
  65.5 1.8 fusion.124
  70.7 9.5 %scatter_custom_fusion = f32[512,256]{1,0:T(8,128)S(1)} fusion(s32[1536]{0:T(1024)} %param.23, f32[1536,256]{1,0:T(8,128)} %copy.39, f32[]{:T(128)} %constant.80.clone.1), kind=kCustom, calls=%fused_computation.153 | custom fusion | flops 393216 | bytes 524800 | tf_op jit(solution)/shard_map/scatter-add | solution.py:79
  83.4 2.0 fusion.118
  88.7 4.6 %gather_fusion.3 = f32[1536,256]{1,0:T(8,128)} fusion(f32[512,256]{1,0:T(8,128)S(1)} %fusion.85, s32[2048]{0:T(1024)S(1)} %get-tuple-element.129), kind=kCustom, calls=%fused_computation.1.clone | custom fusion | bytes 3151872 | tf_op jit(solution)/shard_map/jit(_take)/gather | solution.py:94
  93.3 3.2 %copy.43 = f32[1536,256]{0,1:T(8,128)} copy(f32[1536,256]{1,0:T(8,128)} %gather_fusion.3) | data formatting | bytes 3145728 | tf_op jit(solution)/shard_map/jit(_take)/gather | solution.py:94
  96.5 2.8 %multiply_reduce_fusion = (f32[256]{0:T(256)}, f32[1536]{0:T(1024)S(1)}, f32[1536]{0:T(1024)S(1)}, f32[256]{0:T(256)}) fusion(f32[1536,256]{0,1:T(8,128)} %copy.43, f32[1536,256]{0,1:T(8,128)S(1)} %copy-done.4, f32[1536]{0:T(1024)S(1)} %add_rsqrt_fusion, f32[1536]{0:T(1024)S(1)} %broadcast_multiply_fusion.4, pred[1536]{0:T(1024)(128)(4,1)S(1)} %get-tuple-element.131, ...), kind=kLoop, calls=%fused_computation.27 | loop fusion | flops 3928576 | bytes 3174912 | tf_op jit(solution)/shard_map/reduce_sum | solution.py:41
  100.7 2.3 fusion.117
  103.6 3.5 %multiply_reduce_fusion.1 = (f32[256]{0:T(256)}, f32[1536]{0:T(1024)S(1)}, f32[1536]{0:T(1024)}, f32[256]{0:T(256)}, f32[1536,256]{0,1:T(8,128)}) fusion(f32[1536,256]{0,1:T(8,128)S(1)} %get-tuple-element.108, f32[1536]{0:T(1024)S(1)} %add_rsqrt_fusion.1, f32[1536]{0:T(1024)S(1)} %broadcast_multiply_fusion.5, f32[256]{0:T(256)S(1)} %bitcast.216, ...), kind=kOutput, calls=%fused_computation.28 | convolution fusion | flops 205648384 | bytes 5665280 | tf_op jit(solution)/shard_map/dot_general | solution.py:19
  107.1 9.1 %scatter_custom_fusion.3 = f32[512,256]{1,0:T(8,128)S(1)} fusion(s32[1536]{0:T(1024)} %param.23, bf16[1536,256]{1,0:T(8,128)(2,1)S(1)} %get-tuple-element.76, f32[]{:T(128)} %constant.80.clone.1), kind=kCustom, calls=%fused_computation.19 | custom fusion | flops 786432 | bytes 1311232 | tf_op jit(solution)/shard_map/scatter-add | solution.py:98
  116.3 10.2 %scatter_custom_fusion.1 = f32[1024,256]{1,0:T(8,128)} fusion(s32[1536]{0:T(1024)} %param.22, bf16[1536,256]{1,0:T(8,128)(2,1)S(1)} %get-tuple-element.76, f32[]{:T(128)} %constant.80.clone.1), kind=kCustom, calls=%fused_computation.21 | custom fusion | flops 786432 | bytes 1835520 | tf_op jit(solution)/shard_map/scatter-add | solution.py:97
  126.6 2.6 fusion.48
  129.1 2.1 convolution_convert_fusion
  133.2 2.6 %multiply_reduce_fusion.13 = (f32[256]{0:T(256)}, f32[512]{0:T(512)S(1)}, f32[512]{0:T(512)S(1)}, f32[256]{0:T(256)}, f32[512,256]{0,1:T(8,128)}) fusion(f32[512,256]{0,1:T(8,128)S(1)} %copy-done.7, f32[512]{0:T(512)S(1)} %add_rsqrt_fusion.5, f32[512]{0:T(512)S(1)} %broadcast_multiply_fusion.17, f32[256]{0:T(256)S(1)} %bitcast.212, ...), kind=kOutput, calls=%fused_computation.118 | convolution fusion | flops 68549120 | bytes 2239488 | tf_op jit(solution)/shard_map/dot_general | solution.py:19
  137.0 4.0 %all-to-all-start.1 = ((bf16[16,64,256]{2,1,0:T(8,128)(2,1)}), bf16[16,64,256]{2,1,0:T(8,128)(2,1)}, u32[]{:S(2)}, u32[]{:S(2)}) async-start(bf16[16,64,256]{2,1,0:T(8,128)(2,1)} %bitcast.204), calls=%async_computation.1 | async-start | bytes 1048576 | tf_op jit(solution)/shard_map/all_to_all | solution.py:103
  141.1 1.9 fusion.115
  143.0 2.6 %fusion.128 = (f32[256]{0:T(256)}, bf16[512,256]{1,0:T(8,128)(2,1)}) fusion(f32[512,256]{1,0:T(8,128)S(1)} %copy-done.52, bf16[6,256,256]{2,1,0:T(8,128)(2,1)} %param.30, bf16[512,256]{0,1:T(8,128)(2,1)S(1)} %get-tuple-element.72), kind=kOutput, calls=%fused_computation.266 | convolution fusion | flops 68419328 | bytes 1180672 | tf_op jit(solution)/shard_map/dot_general | solution.py:19
  148.8 2.4 all-to-all-done.1
  151.3 7.3 %scatter_custom_fusion.2 = f32[1024,256]{1,0:T(8,128)S(1)} fusion(f32[1024,256]{1,0:T(8,128)S(1)} %copy-done.10, s32[1024]{0:T(1024)} %reshape.300, bf16[1024,256]{1,0:T(8,128)(2,1)} %bitcast.74), kind=kCustom, calls=%fused_computation.88 | custom fusion | flops 524288 | bytes 1572864 | tf_op jit(solution)/shard_map/scatter-add | solution.py:104
  173.0 1.8 copy.50
  174.8 2.5 fusion.129
  178.3 32.4 %all-reduce = (f32[3,256]{1,0:T(4,128)}, f32[4,256]{1,0:T(4,128)}, f32[6,4,256]{2,1,0:T(4,128)}) all-reduce(f32[3,256]{1,0:T(4,128)S(1)} %convolution_bitcast_fusion.8, f32[4,256]{1,0:T(4,128)S(1)} %convolution_bitcast_fusion.7, f32[6,4,256]{2,1,0:T(4,128)S(1)} %constant_dynamic-update-slice_fusion), channel_id=1, replica_groups=mesh['gp'=16] {'gp'}, use_global_device_ids=true, to_apply=%region_27.29 | all-reduce | flops 7936 | bytes 63488 | tf_op jit(solution)/shard_map/psum | solution.py:116
  211.8 35.2 %all-reduce.4.cloned.1.call-done = (f32[164,256]{1,0:T(8,128)}, f32[768,256]{1,0:T(8,128)}, f32[512,256]{1,0:T(8,128)}, f32[256,256]{1,0:T(8,128)}, f32[6,256,256]{2,1,0:T(8,128)}) async-done(((f32[164,256]{1,0:T(8,128)}, f32[768,256]{1,0:T(8,128)}, f32[512,256]{1,0:T(8,128)}, f32[256,256]{1,0:T(8,128)}, f32[6,256,256]{2,1,0:T(8,128)}), (f32[164,256]{1,0:T(8,128)}, f32[768,256]{1,0:T(8,128)}, ...) | async-done | bytes 3313680 | tf_op jit(solution)/shard_map/psum | solution.py:116
  248.7 2.2 copy.73
  (375 shorter events, 65.9 us)
Async XLA Ops:
  10.3 31.8 %copy-start.72 = (f32[1,1,256]{2,1,0:T(1,128)}, f32[1,1,256]{2,1,0:T(1,128)S(1)}, u32[]{:S(2)}) copy-start(f32[1,1,256]{2,1,0:T(1,128)S(1)} %get-tuple-element.93) | copy-start | bytes 3076
  10.3 31.8 %copy-start.91 = (f32[1,1,256]{2,1,0:T(1,128)}, f32[1,1,256]{2,1,0:T(1,128)S(1)}, u32[]{:S(2)}) copy-start(f32[1,1,256]{2,1,0:T(1,128)S(1)} %get-tuple-element.81) | copy-start | bytes 3076
  13.2 29.0 %copy-start.1 = (f32[1024,256]{0,1:T(8,128)}, f32[1024,256]{0,1:T(8,128)S(1)}, u32[]{:S(2)}) copy-start(f32[1024,256]{0,1:T(8,128)S(1)} %get-tuple-element.110) | copy-start | bytes 3145732
  17.7 6.9 %copy-start.60 = (s32[16,64]{1,0:T(8,128)S(1)}, s32[16,64]{1,0:T(8,128)}, u32[]{:S(2)}) copy-start(s32[16,64]{1,0:T(8,128)} %param.21) | copy-start | bytes 12292
  17.7 9.0 %copy-start.69 = (s32[1536]{0:T(1024)S(1)}, s32[1536]{0:T(1024)}, u32[]{:S(2)}) copy-start(s32[1536]{0:T(1024)} %param.22) | copy-start | bytes 18436
  17.7 9.6 %copy-start.68 = (s32[1536]{0:T(1024)S(1)}, s32[1536]{0:T(1024)}, u32[]{:S(2)}) copy-start(s32[1536]{0:T(1024)} %param.23) | copy-start | bytes 18436
  17.8 12.0 %copy-start.49 = (bf16[256,256]{1,0:T(8,128)(2,1)S(1)}, bf16[256,256]{1,0:T(8,128)(2,1)}, u32[]{:S(2)}) copy-start(bf16[256,256]{1,0:T(8,128)(2,1)} %param.29) | copy-start | bytes 393220
  18.8 37.9 %all-to-all-start = ((bf16[16,64,256]{2,1,0:T(8,128)(2,1)}), bf16[16,64,256]{2,1,0:T(8,128)(2,1)}, u32[]{:S(2)}, u32[]{:S(2)}) async-start(bf16[16,64,256]{2,1,0:T(8,128)(2,1)} %broadcast_select_fusion), calls=%async_computation | async-start | bytes 1048576 | tf_op jit(solution)/shard_map/all_to_all | solution.py:72
  26.7 12.8 %copy-start.74 = (f32[1,1,256]{2,1,0:T(1,128)}, f32[1,1,256]{2,1,0:T(1,128)S(1)}, u32[]{:S(2)}) copy-start(f32[1,1,256]{2,1,0:T(1,128)S(1)} %get-tuple-element.102) | copy-start | bytes 3076
  26.7 12.9 %copy-start.96 = (f32[1,1,256]{2,1,0:T(1,128)}, f32[1,1,256]{2,1,0:T(1,128)S(1)}, u32[]{:S(2)}) copy-start(f32[1,1,256]{2,1,0:T(1,128)S(1)} %get-tuple-element.101) | copy-start | bytes 3076
  29.8 12.3 %copy-start.12 = (bf16[1024,256]{0,1:T(8,128)(2,1)}, bf16[1024,256]{0,1:T(8,128)(2,1)S(1)}, u32[]{:S(2)}) copy-start(bf16[1024,256]{0,1:T(8,128)(2,1)S(1)} %copy.40) | copy-start | bytes 1572868
  31.8 10.4 %copy-start.8 = (f32[1024,256]{0,1:T(8,128)}, f32[1024,256]{0,1:T(8,128)S(1)}, u32[]{:S(2)}) copy-start(f32[1024,256]{0,1:T(8,128)S(1)} %get-tuple-element.117) | copy-start | bytes 3145732
  31.9 10.2 %copy-start.63 = (f32[1024]{0:T(1024)}, f32[1024]{0:T(1024)S(1)}, u32[]{:S(2)}) copy-start(f32[1024]{0:T(1024)S(1)} %add_rsqrt_fusion.2) | copy-start | bytes 12292
  32.2 9.9 %copy-start.84 = (f32[1024]{0:T(1024)}, f32[1024]{0:T(1024)S(1)}, u32[]{:S(2)}) copy-start(f32[1024]{0:T(1024)S(1)} %get-tuple-element.133) | copy-start | bytes 12292
  32.2 9.9 %copy-start.86 = (f32[1024]{0:T(1024)}, f32[1024]{0:T(1024)S(1)}, u32[]{:S(2)}) copy-start(f32[1024]{0:T(1024)S(1)} %get-tuple-element.134) | copy-start | bytes 12292
  70.7 10.9 %copy-start.128 = (f32[1,1,256]{2,1,0:T(1,128)S(1)}, f32[1,1,256]{2,1,0:T(1,128)}, u32[]{:S(2)}) copy-start(f32[1,1,256]{2,1,0:T(1,128)} %get-tuple-element.86) | copy-start | bytes 3076
  126.5 4.7 %copy-start.7 = (f32[512,256]{0,1:T(8,128)S(1)}, f32[512,256]{0,1:T(8,128)}, u32[]{:S(2)}) copy-start(f32[512,256]{0,1:T(8,128)} %copy-done.6) | copy-start | bytes 1572868
  126.5 4.7 %copy-start.20 = (f32[512,256]{0,1:T(8,128)S(1)}, f32[512,256]{0,1:T(8,128)}, u32[]{:S(2)}) copy-start(f32[512,256]{0,1:T(8,128)} %copy-done.19) | copy-start | bytes 1572868
  126.5 4.7 %copy-start.24 = (bf16[512,256]{0,1:T(8,128)(2,1)S(1)}, bf16[512,256]{0,1:T(8,128)(2,1)}, u32[]{:S(2)}) copy-start(bf16[512,256]{0,1:T(8,128)(2,1)} %copy.42) | copy-start | bytes 786436
  126.5 4.7 %copy-start.66 = (f32[512]{0:T(512)S(1)}, f32[512]{0:T(512)}, u32[]{:S(2)}) copy-start(f32[512]{0:T(512)} %copy-done.65) | copy-start | bytes 6148
  126.5 4.7 %copy-start.75 = (f32[1,1,256]{2,1,0:T(1,128)S(1)}, f32[1,1,256]{2,1,0:T(1,128)}, u32[]{:S(2)}) copy-start(f32[1,1,256]{2,1,0:T(1,128)} %copy-done.74) | copy-start | bytes 3076
  126.5 4.7 %copy-start.81 = (f32[512]{0:T(512)S(1)}, f32[512]{0:T(512)}, u32[]{:S(2)}) copy-start(f32[512]{0:T(512)} %copy-done.80) | copy-start | bytes 6148
  126.5 4.7 %copy-start.94 = (f32[1,1,256]{2,1,0:T(1,128)S(1)}, f32[1,1,256]{2,1,0:T(1,128)}, u32[]{:S(2)}) copy-start(f32[1,1,256]{2,1,0:T(1,128)} %get-tuple-element.85) | copy-start | bytes 3076
  126.5 4.7 %copy-start.97 = (f32[1,1,256]{2,1,0:T(1,128)S(1)}, f32[1,1,256]{2,1,0:T(1,128)}, u32[]{:S(2)}) copy-start(f32[1,1,256]{2,1,0:T(1,128)} %copy-done.96) | copy-start | bytes 3076
  126.5 4.7 %copy-start.102 = (f32[512]{0:T(512)S(1)}, f32[512]{0:T(512)}, u32[]{:S(2)}) copy-start(f32[512]{0:T(512)} %copy-done.101) | copy-start | bytes 6148
  126.6 4.7 %copy-start.105 = (f32[512]{0:T(512)S(1)}, f32[512]{0:T(512)}, u32[]{:S(2)}) copy-start(f32[512]{0:T(512)} %copy-done.104) | copy-start | bytes 6148
  135.9 7.1 %copy-start.52 = (f32[512,256]{1,0:T(8,128)S(1)}, f32[512,256]{1,0:T(8,128)}, u32[]{:S(2)}) copy-start(f32[512,256]{1,0:T(8,128)} %copy-done.51) | copy-start | bytes 1572868
  137.0 14.3 %all-to-all-start.1 = ((bf16[16,64,256]{2,1,0:T(8,128)(2,1)}), bf16[16,64,256]{2,1,0:T(8,128)(2,1)}, u32[]{:S(2)}, u32[]{:S(2)}) async-start(bf16[16,64,256]{2,1,0:T(8,128)(2,1)} %bitcast.204), calls=%async_computation.1 | async-start | bytes 1048576 | tf_op jit(solution)/shard_map/all_to_all | solution.py:103
  141.0 106.1 %all-reduce.4.cloned.1.call-start = ((), (), s32[]{:S(2)}) async-start(), calls=%async_computation.2 | async-start | bytes 6635520 | tf_op jit(solution)/shard_map/psum | solution.py:116
  151.3 7.6 %copy-start.2 = (f32[1024,256]{0,1:T(8,128)S(1)}, f32[1024,256]{0,1:T(8,128)}, u32[]{:S(2)}) copy-start(f32[1024,256]{0,1:T(8,128)} %copy-done.1) | copy-start | bytes 3145732
  151.3 7.6 %copy-start.73 = (f32[1,1,256]{2,1,0:T(1,128)S(1)}, f32[1,1,256]{2,1,0:T(1,128)}, u32[]{:S(2)}) copy-start(f32[1,1,256]{2,1,0:T(1,128)} %copy-done.72) | copy-start | bytes 3076
  177.5 33.2 %copy-start.55 = (bf16[164,256]{1,0:T(8,128)(2,1)S(1)}, bf16[164,256]{1,0:T(8,128)(2,1)}, u32[]{:S(2)}) copy-start(bf16[164,256]{1,0:T(8,128)(2,1)} %param.24) | copy-start | bytes 251908
  (106 other events, 206.8 us)
Sparse Core Ops, SparseCore 0:
  171.4 75.5 all-reduce.3
where the time goes:
time: 265 us; the launch traced here: 261 us
  other arithmetic  58.4 us (22%)
  matrix products  56.6 us (21%)
  local copies, waits for them, and re-layouts  49.8 us (19%)
  waiting for transfers between devices  37.7 us (14%)
  blocking collectives  32.4 us (12%)
  between operations  15.9 us (6%)
  starting transfers between devices  9.92 us (4%)
    psum x1, waiting for transfers between devices, local_step(): weight_grads = lax.psum(weight_grads, AXIS_NAME)  35.2 us
    psum x1, blocking collectives, local_step(): weight_grads = lax.psum(weight_grads, AXIS_NAME)  32.4 us
    dot_general x13, matrix products, contract_cols(): lax.dot_general(lhs, rhs, (((1,), (1,)), ((), ())), preferred_element_typ...  25 us
    unnamed x279, local copies, waits for them, and re-layouts  20.9 us
    dot_general x15, matrix products, matmul(): return jnp.dot(lhs, rhs, preferred_element_type=jnp.float32)  19.6 us
    dot_general x15, matrix products, contract_rows(): lax.dot_general(lhs, rhs, (((0,), (0,)), ((), ())), preferred_element_typ...  11.9 us
    scatter-add x1, other arithmetic, local_step(): jax.ops.segment_sum(d_pre3_wide, edge_src, num_segments=slot_rows)  10.2 us
    scatter-add x1, other arithmetic, local_step(): jax.ops.segment_sum(edge_new.astype(jnp.float32), edge_dst, num_segments=...  9.55 us
  transfers between devices with their start and end apart: 3, of which 2 were waited for; matrix products, arithmetic and copies ran while one was open for 18% of the time, Pallas kernels for 0%

commit v1 on v0

v1 whole, which is shorter than its diff:
```python
import functools

import jax
import jax.numpy as jnp
from jax import lax
from jax.experimental import pallas as pl
from jax.experimental.pallas import tpu as pltpu
from jax.sharding import PartitionSpec as P

LN_EPS = 1e-5
AXIS_NAME = 'gp'
N_DEV = 16
N_CHIP = 8
LAT = 256
BLK = 256
F32 = jnp.float32
BF16 = jnp.bfloat16

GROUP_ROWS = (512, 1792, 512, 512)
ROW_EDGE_IN = 168
ROW_MESH_IN = 176
ROW_VEC = 184


def mm(a, b):
    return lax.dot_general(a, b, (((1,), (0,)), ((), ())), preferred_element_type=F32)


def mm_nt(a, b):
    return lax.dot_general(a, b, (((1,), (1,)), ((), ())), preferred_element_type=F32)


def mm_tn(a, b):
    return lax.dot_general(a, b, (((0,), (0,)), ((), ())), preferred_element_type=F32)


def fold8(x):
    return jnp.sum(x.reshape(-1, 8, x.shape[-1]), axis=0)


def main_kernel(
        grid_in, mesh_static, edge_static, send_rows, edge_src, edge_dst,
        w_grid_in, w_mesh_in, w_edge_in, w_edge_up, w_mesh_up, w_grid_up, w_second, vectors, d_mesh_out, d_grid_out,
        mesh_out, grid_out, d_grid_in, res0, res1, res2, res3,
        grid_lat, mesh_lat, edge_lat, outgoing, incoming, d_incoming, d_outgoing,
        oh_src, oht_src, oh_dst, oht_dst,
        hid0, hid1, hid2, hid3, hid4, hid5,
        ds0, ds1, ds2, ds3, nm0, nm1, nm2, nm3, iv0, iv1, iv2, iv3,
        part3, edge_new, agg, d_grid_lat, d_mesh_lat, d_edge_lat, d_agg, d_slot, d_node,
        dl_g, dp_g, dl_m4, dp_m4, dl_e3, dp_e3, dl_e2, dp_e2, dl_m1, dp_m1, dl_g0, dp_g0,
        par0, par1, par2, par3, ra0, ra1, ra2, ra3, cs0, cs1, cs2, cs3, rb0, rb1, rb2, rb3,
        f_send, f_recv, b_send, b_recv, s0_send, s0_recv, s1_send, s1_recv, s2_send, s2_recv, s3_send, s3_recv):
    me = lax.axis_index(AXIS_NAME)
    core = me % 2
    chip = me // 2
    n_grid = grid_lat.shape[0]
    n_mesh = mesh_lat.shape[0]
    n_edge = edge_lat.shape[0]
    slots = send_rows.shape[1]
    pars, ras, css, rbs, ress = (par0, par1, par2, par3), (ra0, ra1, ra2, ra3), (cs0, cs1, cs2, cs3), (rb0, rb1, rb2, rb3), (res0, res1, res2, res3)

    def flip(idx, j):
        out = 0
        for b in range(4):
            bit = (idx // (1 << b)) % 2
            out = out + (1 << b) * (1 - bit if (j >> b) & 1 else bit)
        return out

    barrier = pltpu.get_barrier_semaphore()
    for j in range(1, N_DEV):
        pl.semaphore_signal(barrier, inc=1, device_id=(flip(me, j),), device_id_type=pl.DeviceIdType.MESH)

    pending = []

    def send(src, dst, send_sem, recv_sem, dev):
        copy = pltpu.make_async_remote_copy(src_ref=src, dst_ref=dst, send_sem=send_sem, recv_sem=recv_sem,
                                            device_id=(dev,), device_id_type=pl.DeviceIdType.MESH)
        copy.start()
        pending.append(copy)
        return copy

    far_first = (15, 14, 7, 6, 11, 10, 13, 12, 3, 2, 5, 4, 9, 8, 1)
    chip_order = (7, 3, 5, 6, 1, 2, 4)

    def exchange(src, dst, send_sem, recv_sem):
        copies = []
        for j in far_first:
            peer = flip(me, j)
            copies.append(send(src.at[pl.ds(pl.multiple_of(peer * slots, slots), slots)],
                               dst.at[pl.ds(pl.multiple_of(me * slots, slots), slots)],
                               send_sem.at[j], recv_sem.at[j], peer))
        mine = pl.ds(pl.multiple_of(me * slots, slots), slots)
        dst[mine, :] = src[mine, :]
        return copies

    live = {}

    def stage0(g):
        half = GROUP_ROWS[g] // 2
        other = pl.ds(pl.multiple_of((1 - core) * half, half), half)
        live[g] = [send(pars[g].at[other], ras[g], s0_send.at[g], s0_recv.at[g], flip(me, 1))]

    def stage1(g):
        live[g][0].wait_recv()
        half = GROUP_ROWS[g] // 2
        part = half // N_CHIP
        mine = pl.ds(pl.multiple_of(core * half, half), half)
        total = pars[g][mine, :] + ras[g][...]
        ras[g][...] = total
        css[g][...] = total.astype(BF16)
        copies = []
        for j in chip_order:
            peer = flip(me, 2 * j)
            copies.append(send(css[g].at[pl.ds(pl.multiple_of((peer // 2) * part, part), part)], rbs[g].at[j - 1],
                               s1_send.at[g, j], s1_recv.at[g, j], peer))
        live[g] = copies

    def stage2(g):
        half = GROUP_ROWS[g] // 2
        part = half // N_CHIP
        for copy in live[g]:
            copy.wait_recv()
        total = ras[g][pl.ds(pl.multiple_of(chip * part, part), part), :]
        for j in range(1, N_CHIP):
            total = total + rbs[g][j - 1].astype(F32)
        mine = pl.ds(pl.multiple_of(core * half + chip * part, part), part)
        ress[g][mine, :] = total.astype(BF16)
        copies = []
        for j in chip_order:
            copies.append(send(ress[g].at[mine], ress[g].at[mine], s2_send.at[g, j], s2_recv.at[g, j], flip(me, 2 * j)))
        live[g] = copies

    def stage3(g):
        half = GROUP_ROWS[g] // 2
        for copy in live[g]:
            copy.wait_recv()
        mine = pl.ds(pl.multiple_of(core * half, half), half)
        live[g] = [send(ress[g].at[mine], ress[g].at[mine], s3_send.at[g], s3_recv.at[g], flip(me, 1))]

    def stage4(g):
        live[g][0].wait_recv()

    def blk(i, size=BLK):
        return pl.ds(pl.multiple_of(i * size, size), size)

    def vec(k, i):
        return vectors[k, i:i + 1, :]

    def mlp_fwd(k, pre):
        x = pre + vec(k, 0)
        sig = jax.nn.sigmoid(x)
        act = x * sig
        hid = act.astype(BF16)
        o = mm(hid, w_second[k]) + vec(k, 1)
        cen = o - jnp.mean(o, axis=-1, keepdims=True)
        inv = lax.rsqrt(jnp.mean(cen * cen, axis=-1, keepdims=True) + LN_EPS)
        nrm = cen * inv
        out = nrm * vec(k, 2) + vec(k, 3)
        dsilu = sig + act * (1.0 - sig)
        return out, hid, dsilu, nrm, inv

    def mlp_bwd(k, dsilu, nrm, inv, d_out):
        dn = d_out * vec(k, 2)
        m1 = jnp.mean(dn, axis=-1, keepdims=True)
        m2 = jnp.mean(dn * nrm, axis=-1, keepdims=True)
        d_lin = inv * (dn - m1 - nrm * m2)
        d_lin_bf = d_lin.astype(BF16)
        d_pre = mm_nt(d_lin_bf, w_second[k]) * dsilu
        return d_lin_bf, d_pre.astype(BF16), (fold8(d_pre), fold8(d_lin), fold8(d_out * nrm), fold8(d_out))

    zeros4 = tuple(jnp.zeros((8, LAT), F32) for _ in range(4))

    def put_vec(k, sums):
        for i in range(4):
            par3[256 + ROW_VEC + 4 * k + i:256 + ROW_VEC + 4 * k + i + 1, :] = jnp.sum(sums[i], axis=0, keepdims=True)

    def add4(a, b):
        return tuple(x + y for x, y in zip(a, b))

    par3[256:512, :] = jnp.zeros((256, LAT), F32)

    def grid_embed(i, c):
        rows = blk(i)
        out, hid, dsilu, nrm, inv = mlp_fwd(0, mm(grid_in[rows, :], w_grid_in[...]))
        grid_lat[rows, :] = out.astype(BF16)
        hid0[rows, :] = hid
        ds0[rows, :] = dsilu
        nm0[rows, :] = nrm
        iv0[rows, :] = inv
        return c

    lax.fori_loop(0, n_grid // BLK, grid_embed, 0)

    def row_pair(i):
        return jnp.concatenate([send_rows[2 * i:2 * i + 1, :], send_rows[2 * i + 1:2 * i + 2, :]], axis=1)

    def columns_of(row):
        return jnp.transpose(jnp.broadcast_to(row, (128, 128)))

    def one_hot(col, n):
        lane = lax.broadcasted_iota(jnp.int32, (128, 128), 1)
        return jnp.concatenate([jnp.where(col - 128 * t == lane, 1.0, 0.0).astype(BF16) for t in range(n // 128)], axis=1)

    def one_hot_t(row, n):
        sub = lax.broadcasted_iota(jnp.int32, (n, 128), 0)
        return jnp.where(sub == row, 1.0, 0.0).astype(BF16)

    for i in range(N_DEV // 2):
        pick = one_hot(columns_of(row_pair(i)), n_grid)
        outgoing[128 * i:128 * (i + 1), :] = mm(pick, grid_lat[...]).astype(BF16)

    pl.semaphore_wait(barrier, N_DEV - 1)
    fwd = exchange(outgoing, incoming, f_send, f_recv)

    def grid_update(i, sums):
        rows = blk(i)
        lat = grid_lat[rows, :]
        out, hid, dsilu, nrm, inv = mlp_fwd(5, mm(lat, w_grid_up[...]))
        grid_out[rows, :] = (lat.astype(F32) + out).astype(BF16)
        d_out = d_grid_out[rows, :].astype(F32)
        d_lin, d_pre, add = mlp_bwd(5, dsilu, nrm, inv, d_out)
        hid5[rows, :] = hid
        dl_g[rows, :] = d_lin
        dp_g[rows, :] = d_pre
        d_grid_lat[rows, :] = d_out + mm_nt(d_pre, w_grid_up[...])
        return add4(sums, add)

    put_vec(5, lax.fori_loop(0, n_grid // BLK, grid_update, zeros4))
    par0[0:256, :] = mm_tn(grid_lat[...], dp_g[...])
    par0[256:512, :] = mm_tn(hid5[...], dl_g[...])
    stage0(0)

    def mesh_embed(i, c):
        rows = blk(i)
        out, hid, dsilu, nrm, inv = mlp_fwd(1, mm(mesh_static[rows, :], w_mesh_in[...]))
        mesh_lat[rows, :] = out.astype(BF16)
        hid1[rows, :] = hid
        ds1[rows, :] = dsilu
        nm1[rows, :] = nrm
        iv1[rows, :] = inv
        return c

    lax.fori_loop(0, n_mesh // BLK, mesh_embed, 0)

    def hots(i, c):
        rows = blk(i, 128)
        src = edge_src[pl.ds(i, 1), :]
        dst = edge_dst[pl.ds(i, 1), :]
        oh_src[rows, :] = one_hot(columns_of(src), n_grid)
        oh_dst[rows, :] = one_hot(columns_of(dst), n_mesh)
        oht_src[:, rows] = one_hot_t(src, n_grid)
        oht_dst[:, rows] = one_hot_t(dst, n_mesh)
        return c

    lax.fori_loop(0, n_edge // 128, hots, 0)
    stage1(0)

    def edge_embed(i, c):
        rows = blk(i)
        out, hid, dsilu, nrm, inv = mlp_fwd(2, mm(edge_static[rows, :], w_edge_in[...]))
        lat = out.astype(BF16)
        edge_lat[rows, :] = lat
        hid2[rows, :] = hid
        ds2[rows, :] = dsilu
        nm2[rows, :] = nrm
        iv2[rows, :] = inv
        recv = mm(oh_dst[rows, :], mesh_lat[...]).astype(BF16)
        part3[rows, :] = mm(lat, w_edge_up[0:LAT, :]) + mm(recv, w_edge_up[2 * LAT:3 * LAT, :])
        return c

    lax.fori_loop(0, n_edge // BLK, edge_embed, 0)
    stage2(0)

    for copy in fwd:
        copy.wait_recv()

    def edge_update(i, c):
        rows = blk(i)
        sender = mm(oh_src[rows, :], incoming[...]).astype(BF16)
        out, hid, dsilu, nrm, inv = mlp_fwd(3, part3[rows, :] + mm(sender, w_edge_up[LAT:2 * LAT, :]))
        edge_new[rows, :] = (edge_lat[rows, :].astype(F32) + out).astype(BF16)
        hid3[rows, :] = hid
        ds3[rows, :] = dsilu
        nm3[rows, :] = nrm
        iv3[rows, :] = inv
        return c

    lax.fori_loop(0, n_edge // BLK, edge_update, 0)
    stage3(0)

    def mesh_update(i, sums):
        rows = blk(i)
        total = mm(oht_dst[rows, :], edge_new[...]).astype(BF16)
        agg[rows, :] = total
        lat = mesh_lat[rows, :]
        out, hid, dsilu, nrm, inv = mlp_fwd(4, mm(lat, w_mesh_up[0:LAT, :]) + mm(total, w_mesh_up[LAT:2 * LAT, :]))
        mesh_out[rows, :] = (lat.astype(F32) + out).astype(BF16)
        d_out = d_mesh_out[rows, :].astype(F32)
        d_lin, d_pre, add = mlp_bwd(4, dsilu, nrm, inv, d_out)
        hid4[rows, :] = hid
        dl_m4[rows, :] = d_lin
        dp_m4[rows, :] = d_pre
        d_mesh_lat[rows, :] = d_out + mm_nt(d_pre, w_mesh_up[0:LAT, :])
        d_agg[rows, :] = mm_nt(d_pre, w_mesh_up[LAT:2 * LAT, :]).astype(BF16)
        return add4(sums, add)

    put_vec(4, lax.fori_loop(0, n_mesh // BLK, mesh_update, zeros4))

    def edge_back(i, sums):
        rows = blk(i)
        d_out = mm(oh_dst[rows, :], d_agg[...])
        d_lin, d_pre, add = mlp_bwd(3, ds3[rows, :], nm3[rows, :], iv3[rows, :], d_out)
        dl_e3[rows, :] = d_lin
        dp_e3[rows, :] = d_pre
        d_edge_lat[rows, :] = d_out + mm_nt(d_pre, w_edge_up[0:LAT, :])
        return add4(sums, add)

    put_vec(3, lax.fori_loop(0, n_edge // BLK, edge_back, zeros4))

    def slot_back(i, c):
        rows = blk(i)
        d_sum = mm(oht_src[rows, :], dp_e3[...]).astype(BF16)
        d_slot[rows, :] = d_sum
        d_incoming[rows, :] = mm_nt(d_sum, w_edge_up[LAT:2 * LAT, :]).astype(BF16)
        return c

    lax.fori_loop(0, n_grid // BLK, slot_back, 0)
    bwd = exchange(d_incoming, d_outgoing, b_send, b_recv)

    def node_back(i, c):
        rows = blk(i)
        d_sum = mm(oht_dst[rows, :], dp_e3[...]).astype(BF16)
        d_node[rows, :] = d_sum
        d_mesh_lat[rows, :] = d_mesh_lat[rows, :] + mm_nt(d_sum, w_edge_up[2 * LAT:3 * LAT, :])
        return c

    lax.fori_loop(0, n_mesh // BLK, node_back, 0)
    par1[0:256, :] = mm_tn(edge_lat[...], dp_e3[...])
    par1[256:512, :] = mm_tn(incoming[...], d_slot[...])
    par1[512:768, :] = mm_tn(mesh_lat[...], d_node[...])
    par1[768:1024, :] = mm_tn(hid3[...], dl_e3[...])
    par1[1024:1280, :] = mm_tn(mesh_lat[...], dp_m4[...])
    par1[1280:1536, :] = mm_tn(agg[...], dp_m4[...])
    par1[1536:1792, :] = mm_tn(hid4[...], dl_m4[...])
    stage0(1)

    def mesh_in_back(i, sums):
        rows = blk(i)
        d_lin, d_pre, add = mlp_bwd(1, ds1[rows, :], nm1[rows, :], iv1[rows, :], d_mesh_lat[rows, :])
        dl_m1[rows, :] = d_lin
        dp_m1[rows, :] = d_pre
        return add4(sums, add)

    put_vec(1, lax.fori_loop(0, n_mesh // BLK, mesh_in_back, zeros4))
    stage1(1)

    def edge_in_back(i, sums):
        rows = blk(i)
        d_lin, d_pre, add = mlp_bwd(2, ds2[rows, :], nm2[rows, :], iv2[rows, :], d_edge_lat[rows, :])
        dl_e2[rows, :] = d_lin
        dp_e2[rows, :] = d_pre
        return add4(sums, add)

    put_vec(2, lax.fori_loop(0, n_edge // BLK, edge_in_back, zeros4))
    par2[0:256, :] = mm_tn(hid2[...], dl_e2[...])
    par2[256:512, :] = mm_tn(hid1[...], dl_m1[...])
    stage0(2)
    par3[256 + ROW_EDGE_IN:256 + ROW_EDGE_IN + 4, :] = mm_tn(edge_static[...], dp_e2[...])
    par3[256 + ROW_MESH_IN:256 + ROW_MESH_IN + 3, :] = mm_tn(mesh_static[...], dp_m1[...])
    stage2(1)

    for copy in bwd:
        copy.wait_recv()

    all_rows = jnp.concatenate([row_pair(i) for i in range(N_DEV // 2)], axis=1)

    def grid_in_back(i, sums):
        rows = blk(i)
        sub = lax.broadcasted_iota(jnp.int32, (BLK, N_DEV * slots), 0) + i * BLK
        spread = jnp.where(sub == all_rows, 1.0, 0.0).astype(BF16)
        d_out = d_grid_lat[rows, :] + mm(spread, d_outgoing[...])
        d_lin, d_pre, add = mlp_bwd(0, ds0[rows, :], nm0[rows, :], iv0[rows, :], d_out)
        dl_g0[rows, :] = d_lin
        dp_g0[rows, :] = d_pre
        d_grid_in[rows, :] = mm_nt(d_pre, w_grid_in[...])
        return add4(sums, add)

    put_vec(0, lax.fori_loop(0, n_grid // BLK, grid_in_back, zeros4))
    par3[0:256, :] = mm_tn(hid0[...], dl_g0[...])
    par3[256:256 + grid_in.shape[1], :] = mm_tn(grid_in[...], dp_g0[...])
    stage0(3)
    stage1(2)
    stage3(1)
    stage1(3)
    stage2(2)
    stage2(3)
    stage3(2)
    stage3(3)
    for g in range(4):
        stage4(g)
    for copy in pending:
        copy.wait_send()


def final_kernel(mesh_res, grid_res, d_grid_res, res0, res1, res2, res3,
                 mesh_out, grid_out, d_grid_in, d_w_grid_in, d_w_mesh_in, d_w_edge_in, d_w_edge_up, d_w_mesh_up, d_w_grid_up, d_w_second, d_vectors):
    mesh_out[...] = mesh_res[...]
    grid_out[...] = grid_res[...]
    d_grid_in[...] = d_grid_res[...]
    d_w_grid_up[...] = res0[0:256, :].astype(F32)
    d_w_second[5] = res0[256:512, :].astype(F32)
    d_w_edge_up[...] = res1[0:768, :].astype(F32)
    d_w_second[3] = res1[768:1024, :].astype(F32)
    d_w_mesh_up[...] = res1[1024:1536, :].astype(F32)
    d_w_second[4] = res1[1536:1792, :].astype(F32)
    d_w_second[2] = res2[0:256, :].astype(F32)
    d_w_second[1] = res2[256:512, :].astype(F32)
    d_w_second[0] = res3[0:256, :].astype(F32)
    small = res3[256:512, :].astype(F32)
    d_w_grid_in[...] = small[0:d_w_grid_in.shape[0], :]
    d_w_edge_in[...] = small[ROW_EDGE_IN:ROW_EDGE_IN + 4, :]
    d_w_mesh_in[...] = small[ROW_MESH_IN:ROW_MESH_IN + 3, :]
    d_vectors[...] = small[ROW_VEC:ROW_VEC + 24, :].reshape(6, 4, LAT)


def solution(mesh):
    row_spec = P(AXIS_NAME, None)
    edge_spec = P(AXIS_NAME)
    rep_spec = P()
    in_specs = (row_spec, row_spec, row_spec, row_spec, edge_spec, edge_spec) + (rep_spec,) * 8 + (row_spec, row_spec)
    out_specs = (row_spec, row_spec, row_spec) + (rep_spec,) * 8

    def local_step(grid_in, mesh_static, edge_static, send_rows, edge_src, edge_dst, *rest):
        n_grid, feats = grid_in.shape
        n_mesh = mesh_static.shape[0]
        n_edge = edge_static.shape[0]
        n_slot = send_rows.size
        src2 = edge_src.reshape(n_edge // 128, 128)
        dst2 = edge_dst.reshape(n_edge // 128, 128)

        def vm(shape, dtype):
            return pltpu.VMEM(shape, dtype)

        def rows_bf(n):
            return vm((n, LAT), BF16)

        def rows_f32(n):
            return vm((n, LAT), F32)

        dma = pltpu.SemaphoreType.DMA
        scratch = [
            rows_bf(n_grid), rows_bf(n_mesh), rows_bf(n_edge), rows_bf(n_slot), rows_bf(n_slot), rows_bf(n_slot), rows_bf(n_slot),
            vm((n_edge, n_slot), BF16), vm((n_slot, n_edge), BF16), vm((n_edge, n_mesh), BF16), vm((n_mesh, n_edge), BF16),
            rows_bf(n_grid), rows_bf(n_mesh), rows_bf(n_edge), rows_bf(n_edge), rows_bf(n_mesh), rows_bf(n_grid),
            rows_f32(n_grid), rows_f32(n_mesh), rows_f32(n_edge), rows_f32(n_edge),
            rows_f32(n_grid), rows_f32(n_mesh), rows_f32(n_edge), rows_f32(n_edge),
            vm((n_grid, 1), F32), vm((n_mesh, 1), F32), vm((n_edge, 1), F32), vm((n_edge, 1), F32),
            rows_f32(n_edge), rows_bf(n_edge), rows_bf(n_mesh), rows_f32(n_grid), rows_f32(n_mesh), rows_f32(n_edge), rows_bf(n_mesh), rows_bf(n_slot), rows_bf(n_mesh),
            rows_bf(n_grid), rows_bf(n_grid), rows_bf(n_mesh), rows_bf(n_mesh), rows_bf(n_edge), rows_bf(n_edge), rows_bf(n_edge), rows_bf(n_edge), rows_bf(n_mesh), rows_bf(n_mesh), rows_bf(n_grid), rows_bf(n_grid),
        ]
        scratch += [rows_f32(r) for r in GROUP_ROWS]
        scratch += [rows_f32(r // 2) for r in GROUP_ROWS]
        scratch += [rows_bf(r // 2) for r in GROUP_ROWS]
        scratch += [vm((7, r // 16, LAT), BF16) for r in GROUP_ROWS]
        scratch += [dma((16,)), dma((16,)), dma((16,)), dma((16,)), dma((4,)), dma((4,)), dma((4, 8)), dma((4, 8)), dma((4, 8)), dma((4, 8)), dma((4,)), dma((4,))]
        shape = jax.ShapeDtypeStruct
        outs = (shape((n_mesh, LAT), BF16), shape((n_grid, LAT), BF16), shape((n_grid, feats), F32)) + tuple(shape((r, LAT), BF16) for r in GROUP_ROWS)
        vspec = pl.BlockSpec(memory_space=pltpu.VMEM)
        results = pl.pallas_call(
            main_kernel,
            out_shape=outs,
            in_specs=[vspec] * 16,
            out_specs=tuple([vspec] * len(outs)),
            scratch_shapes=scratch,
            compiler_params=pltpu.CompilerParams(collective_id=0, has_side_effects=True, vmem_limit_bytes=63 * 1024 * 1024),
        )(grid_in, mesh_static, edge_static, send_rows, src2, dst2, *rest)

        finals = (shape((n_mesh, LAT), BF16), shape((n_grid, LAT), BF16), shape((n_grid, feats), F32),
                  shape((feats, LAT), F32), shape((3, LAT), F32), shape((4, LAT), F32), shape((3 * LAT, LAT), F32),
                  shape((2 * LAT, LAT), F32), shape((LAT, LAT), F32), shape((6, LAT, LAT), F32), shape((6, 4, LAT), F32))
        return pl.pallas_call(
            final_kernel,
            out_shape=finals,
            in_specs=[vspec] * len(outs),
            out_specs=tuple([vspec] * len(finals)),
        )(*results)

    return jax.shard_map(local_step, mesh=mesh, in_specs=in_specs, out_specs=out_specs, check_vma=False)
```

time: 265 us -> 79.7 us (0.30); the launches traced: 261 us -> 79.4 us
  Pallas kernels: 0 us -> 71.3 us
  other arithmetic: 58.4 us -> 0 us
  matrix products: 56.6 us -> 0 us
  local copies, waits for them, and re-layouts: 49.8 us -> 7.53 us
  waiting for transfers between devices: 37.7 us -> 0 us
  blocking collectives: 32.4 us -> 0 us
  between operations: 15.9 us -> 0.65 us
  starting transfers between devices: 9.92 us -> 0 us
    pallas_call x0 -> x2, Pallas kernels: none -> 71.3 us  [the longest x1 67 us: local_step(): pl.pallas_call(main_kernel, out_shape=outs, in_specs=[vspec] * 16, out_sp...]
    dot_general x43 -> x0, matrix products: 56.6 us -> none  [the longest x13 25 us: contract_cols(): lax.dot_general(lhs, rhs, (((1,), (1,)), ((), ())), preferred_element_typ...]
    scatter-add x4 -> x0, other arithmetic: 36.1 us -> none  [the longest x1 10.2 us: local_step(): jax.ops.segment_sum(d_pre3_wide, edge_src, num_segments=slot_rows)]
    psum x1 -> x0, waiting for transfers between devices: 35.2 us -> none  [local_step(): weight_grads = lax.psum(weight_grads, AXIS_NAME)]
    psum x1 -> x0, blocking collectives: 32.4 us -> none  [local_step(): weight_grads = lax.psum(weight_grads, AXIS_NAME)]
    gather x5 -> x0, local copies, waits for them, and re-layouts: 21.1 us -> none  [the longest x2 7.8 us: local_step(): d_edge_new = jnp.take(d_agg, edge_dst, axis=0)]
    unnamed x279 -> x3, local copies, waits for them, and re-layouts: 20.9 us -> 5.14 us
    reduce_sum x17 -> x0, other arithmetic: 13.5 us -> none  [the longest x6 8.8 us: mlp_tail_back(): jnp.sum(d_lin, axis=0)]
  transfers between devices with their start and end apart: 3 -> 0, of which waited for: 2 -> 0; matrix products, arithmetic and copies ran while one was open for 18% -> 0% of each run, Pallas kernels for 0% -> 0%
where the time goes in v1:
time: 79.7 us; the launch traced here: 79.4 us
  Pallas kernels  71.3 us (89%)
  local copies, waits for them, and re-layouts  7.53 us (9%)
    pallas_call x1, Pallas kernels, local_step(): pl.pallas_call(main_kernel, out_shape=outs, in_specs=[vspec] * 16, out_sp...  67 us
    unnamed x3, local copies, waits for them, and re-layouts  5.14 us
    pallas_call x1, Pallas kernels, local_step(): pl.pallas_call(final_kernel, out_shape=finals, in_specs=[vspec] * len(out...  4.3 us
    pallas_call x1, local copies, waits for them, and re-layouts, local_step(): pl.pallas_call(final_kernel, out_shape=finals, in_specs=[vspec] * len(out...  2.38 us

profile of v1, /device:TPU:0, one launch (start us, length us, event | category | flops | bytes accessed | tf_op | source)
XLA Modules:
  0.0 79.4 jit_solution(18042317868264754238)
XLA Ops:
  0.6 1.5 %copy.28.mesh_static = bf16[512,3]{1,0:T(8,128)(2,1)} copy(bf16[512,3]{0,1:T(4,128)(2,1)} %param.17) | data formatting | bytes 6144 | tf_op args[1]
  2.1 1.7 %copy.29.edge_static = bf16[1536,4]{1,0:T(8,128)(2,1)} copy(bf16[1536,4]{0,1:T(4,128)(2,1)} %param.18) | data formatting | bytes 24576 | tf_op args[2]
  3.8 2.0 %copy.27.grid_in = bf16[1024,164]{1,0:T(8,128)(2,1)} copy(bf16[1024,164]{0,1:T(8,128)(2,1)} %param.16) | data formatting | bytes 671744 | tf_op args[0]
  5.8 67.0 %shard_map.239 = (bf16[512,256]{1,0:T(8,128)(2,1)}, bf16[1024,256]{1,0:T(8,128)(2,1)}, f32[1024,164]{1,0:T(8,128)}, bf16[512,256]{1,0:T(8,128)(2,1)}, bf16[1792,...) custom-call(bf16[1024,164]{1,0:T(8,128)(2,1)} %copy.27.grid_in, ...), custom_call_target="tpu_custom_call" | custom-call | tf_op jit(solution)/shard_map/pallas_call | solution.py:469
  72.7 4.3 %shard_map.240 = (bf16[512,256]{1,0:T(8,128)(2,1)}, bf16[1024,256]{1,0:T(8,128)(2,1)}, f32[1024,164]{1,0:T(8,128)}, f32[164,256]{1,0:T(8,128)}, f32[3,256]{1,0:T...) custom-call(bf16[512,256]{1,0:T(8,128)(2,1)} %get-tuple-element.18.m, ...), custom_call_target="tpu_custom_call" | custom-call | tf_op jit(solution)/shard_map/pallas_call | solution.py:481
  77.0 2.4 %copy.30 = f32[1024,164]{0,1:T(8,128)} copy(f32[1024,164]{1,0:T(8,128)} %get-tuple-element.27) | data formatting | bytes 1343488 | tf_op jit(solution)/shard_map/pallas_call | solution.py:481

commit v2 on v1

v2 whole, which is shorter than its diff:
```python
import functools

import jax
import jax.numpy as jnp
from jax import lax
from jax.experimental import pallas as pl
from jax.experimental.pallas import tpu as pltpu
from jax.sharding import PartitionSpec as P

LN_EPS = 1e-5
AXIS_NAME = 'gp'
N_DEV = 16
N_CHIP = 8
LAT = 256
BLK_G, BLK_M, BLK_E, BLK_S = 1024, 512, 768, 1024
F32 = jnp.float32
BF16 = jnp.bfloat16

GROUP_ROWS = (512, 768, 1024, 512, 512)
N_GROUP = len(GROUP_ROWS)
ROW_EDGE_IN = 168
ROW_MESH_IN = 176
ROW_VEC = 184


def mm(a, b):
    return lax.dot_general(a, b, (((1,), (0,)), ((), ())), preferred_element_type=F32)


def mm_nt(a, b):
    return lax.dot_general(a, b, (((1,), (1,)), ((), ())), preferred_element_type=F32)


def mm_tn(a, b):
    return lax.dot_general(a, b, (((0,), (0,)), ((), ())), preferred_element_type=F32)


def fold8(x):
    return jnp.sum(x.reshape(-1, 8, x.shape[-1]), axis=0)


def main_kernel(
        grid_in, mesh_static, edge_static, send_rows, edge_src, edge_dst,
        w_grid_in, w_mesh_in, w_edge_in, w_edge_up, w_mesh_up, w_grid_up, w_second, vectors, d_mesh_out, d_grid_out,
        mesh_out, grid_out, d_grid_in, res0, res1, res2, res3, res4,
        grid_lat, mesh_lat, edge_lat, outgoing, incoming, d_incoming, d_outgoing,
        oh_src, oht_src, oh_dst, oht_dst,
        hid0, hid1, hid2, hid3, hid4, hid5,
        ds0, ds1, ds2, ds3, nm0, nm1, nm2, nm3, iv0, iv1, iv2, iv3,
        part3, edge_new, agg, d_grid_lat, d_mesh_lat, d_agg, d_slot, d_node,
        dl_g, dp_g, dl_m, dp_m, dl_e, dp_e,
        par0, par1, par2, par3, par4, ra0, ra1, ra2, ra3, ra4, cs0, cs1, cs2, cs3, cs4, rb0, rb1, rb2, rb3, rb4,
        f_send, f_recv, b_send, b_recv, s0_send, s0_recv, s1_send, s1_recv, s2_send, s2_recv, s3_send, s3_recv):
    me = lax.axis_index(AXIS_NAME)
    core = me % 2
    chip = me // 2
    n_grid = grid_lat.shape[0]
    n_mesh = mesh_lat.shape[0]
    n_edge = edge_lat.shape[0]
    slots = send_rows.shape[1]
    pars, ras, css = (par0, par1, par2, par3, par4), (ra0, ra1, ra2, ra3, ra4), (cs0, cs1, cs2, cs3, cs4)
    rbs, ress = (rb0, rb1, rb2, rb3, rb4), (res0, res1, res2, res3, res4)

    def flip(idx, j):
        out = 0
        for b in range(4):
            bit = (idx // (1 << b)) % 2
            out = out + (1 << b) * (1 - bit if (j >> b) & 1 else bit)
        return out

    def loop(name, lo, hi, body, init):
        with jax.named_scope(name):
            return lax.fori_loop(lo, hi, body, init)

    barrier = pltpu.get_barrier_semaphore()
    for j in range(1, N_DEV):
        pl.semaphore_signal(barrier, inc=1, device_id=(flip(me, j),), device_id_type=pl.DeviceIdType.MESH)

    pending = []

    def send(src, dst, send_sem, recv_sem, dev):
        copy = pltpu.make_async_remote_copy(src_ref=src, dst_ref=dst, send_sem=send_sem, recv_sem=recv_sem,
                                            device_id=(dev,), device_id_type=pl.DeviceIdType.MESH)
        copy.start()
        pending.append(copy)
        return copy

    far_first = (15, 14, 7, 6, 11, 10, 13, 12, 3, 2, 5, 4, 9, 8, 1)
    chip_order = (7, 3, 5, 6, 1, 2, 4)

    def exchange(src, dst, send_sem, recv_sem):
        copies = []
        for j in far_first:
            peer = flip(me, j)
            copies.append(send(src.at[pl.ds(pl.multiple_of(peer * slots, slots), slots)],
                               dst.at[pl.ds(pl.multiple_of(me * slots, slots), slots)],
                               send_sem.at[j], recv_sem.at[j], peer))
        mine = pl.ds(pl.multiple_of(me * slots, slots), slots)
        dst[mine, :] = src[mine, :]
        return copies

    live = {}

    def stage0(g):
        half = GROUP_ROWS[g] // 2
        other = pl.ds(pl.multiple_of((1 - core) * half, half), half)
        live[g] = [send(pars[g].at[other], ras[g], s0_send.at[g], s0_recv.at[g], flip(me, 1))]

    def stage1(g):
        with jax.named_scope('s1_%d' % g):
            live[g][0].wait_recv()
            half = GROUP_ROWS[g] // 2
            part = half // N_CHIP
            mine = pl.ds(pl.multiple_of(core * half, half), half)
            total = pars[g][mine, :] + ras[g][...]
            ras[g][...] = total
            css[g][...] = total.astype(BF16)
            copies = []
            for j in chip_order:
                peer = flip(me, 2 * j)
                copies.append(send(css[g].at[pl.ds(pl.multiple_of((peer // 2) * part, part), part)], rbs[g].at[j - 1],
                                   s1_send.at[g, j], s1_recv.at[g, j], peer))
            live[g] = copies

    def stage2(g):
        with jax.named_scope('s2_%d' % g):
            half = GROUP_ROWS[g] // 2
            part = half // N_CHIP
            for copy in live[g]:
                copy.wait_recv()
            total = ras[g][pl.ds(pl.multiple_of(chip * part, part), part), :]
            for j in range(1, N_CHIP):
                total = total + rbs[g][j - 1].astype(F32)
            mine = pl.ds(pl.multiple_of(core * half + chip * part, part), part)
            ress[g][mine, :] = total.astype(BF16)
            copies = []
            for j in chip_order:
                copies.append(send(ress[g].at[mine], ress[g].at[mine], s2_send.at[g, j], s2_recv.at[g, j], flip(me, 2 * j)))
            live[g] = copies

    def stage3(g):
        with jax.named_scope('s3_%d' % g):
            half = GROUP_ROWS[g] // 2
            for copy in live[g]:
                copy.wait_recv()
            mine = pl.ds(pl.multiple_of(core * half, half), half)
            live[g] = [send(ress[g].at[mine], ress[g].at[mine], s3_send.at[g], s3_recv.at[g], flip(me, 1))]

    def stage4(g):
        with jax.named_scope('s4_%d' % g):
            live[g][0].wait_recv()

    def blk(i, size):
        return pl.ds(pl.multiple_of(i * size, size), size)

    def vec(k, i):
        return vectors[k, i:i + 1, :]

    def mlp_fwd(k, pre):
        x = pre + vec(k, 0)
        sig = jax.nn.sigmoid(x)
        act = x * sig
        hid = act.astype(BF16)
        o = mm(hid, w_second[k]) + vec(k, 1)
        cen = o - jnp.mean(o, axis=-1, keepdims=True)
        inv = lax.rsqrt(jnp.mean(cen * cen, axis=-1, keepdims=True) + LN_EPS)
        nrm = cen * inv
        out = nrm * vec(k, 2) + vec(k, 3)
        dsilu = sig + act * (1.0 - sig)
        return out, hid, dsilu, nrm, inv

    def mlp_bwd(k, dsilu, nrm, inv, d_out):
        dn = d_out * vec(k, 2)
        m1 = jnp.mean(dn, axis=-1, keepdims=True)
        m2 = jnp.mean(dn * nrm, axis=-1, keepdims=True)
        d_lin = inv * (dn - m1 - nrm * m2)
        d_lin_bf = d_lin.astype(BF16)
        d_pre = mm_nt(d_lin_bf, w_second[k]) * dsilu
        return d_lin_bf, d_pre.astype(BF16), (fold8(d_pre), fold8(d_lin), fold8(d_out * nrm), fold8(d_out))

    zeros4 = tuple(jnp.zeros((8, LAT), F32) for _ in range(4))

    def put_vec(k, sums):
        for i in range(4):
            par4[256 + ROW_VEC + 4 * k + i:256 + ROW_VEC + 4 * k + i + 1, :] = jnp.sum(sums[i], axis=0, keepdims=True)

    def add4(a, b):
        return tuple(x + y for x, y in zip(a, b))

    par4[256:512, :] = jnp.zeros((256, LAT), F32)

    def grid_embed(i, c):
        rows = blk(i, BLK_G)
        out, hid, dsilu, nrm, inv = mlp_fwd(0, mm_tn(grid_in[:, rows], w_grid_in[...]))
        grid_lat[rows, :] = out.astype(BF16)
        hid0[rows, :] = hid
        ds0[rows, :] = dsilu
        nm0[rows, :] = nrm
        iv0[rows, :] = inv
        return c

    loop('grid_embed', 0, n_grid // BLK_G, grid_embed, 0)

    def row_pair(i):
        return jnp.concatenate([send_rows[2 * i:2 * i + 1, :], send_rows[2 * i + 1:2 * i + 2, :]], axis=1)

    def columns_of(row):
        return jnp.transpose(jnp.broadcast_to(row, (128, 128)))

    def one_hot(col, n):
        lane = lax.broadcasted_iota(jnp.int32, (128, 128), 1).astype(jnp.int16)
        col = col.astype(jnp.int16)
        return jnp.concatenate([jnp.where(col == lane + jnp.full((), 128 * t, jnp.int16), jnp.ones((), BF16), jnp.zeros((), BF16)) for t in range(n // 128)], axis=1)

    def one_hot_t(row, n):
        sub = lax.broadcasted_iota(jnp.int32, (n, 128), 0).astype(jnp.int16)
        return jnp.where(sub == jnp.broadcast_to(row, (n, 128)).astype(jnp.int16), jnp.ones((), BF16), jnp.zeros((), BF16))

    for i in range(N_DEV // 2):
        pick = one_hot(columns_of(row_pair(i)), n_grid)
        outgoing[128 * i:128 * (i + 1), :] = mm(pick, grid_lat[...]).astype(BF16)

    with jax.named_scope('w_bar'):
        pl.semaphore_wait(barrier, N_DEV - 1)
    fwd = exchange(outgoing, incoming, f_send, f_recv)

    def grid_update(i, sums):
        rows = blk(i, BLK_G)
        lat = grid_lat[rows, :]
        out, hid, dsilu, nrm, inv = mlp_fwd(5, mm(lat, w_grid_up[...]))
        grid_out[rows, :] = (lat.astype(F32) + out).astype(BF16)
        d_out = d_grid_out[rows, :].astype(F32)
        d_lin, d_pre, add = mlp_bwd(5, dsilu, nrm, inv, d_out)
        hid5[rows, :] = hid
        dl_g[rows, :] = d_lin
        dp_g[rows, :] = d_pre
        d_grid_lat[rows, :] = d_out + mm_nt(d_pre, w_grid_up[...])
        return add4(sums, add)

    put_vec(5, loop('grid_update', 0, n_grid // BLK_G, grid_update, zeros4))
    par0[0:256, :] = mm_tn(grid_lat[...], dp_g[...])
    par0[256:512, :] = mm_tn(hid5[...], dl_g[...])
    stage0(0)

    def mesh_embed(i, c):
        rows = blk(i, BLK_M)
        out, hid, dsilu, nrm, inv = mlp_fwd(1, mm_tn(mesh_static[:, rows], w_mesh_in[...]))
        mesh_lat[rows, :] = out.astype(BF16)
        hid1[rows, :] = hid
        ds1[rows, :] = dsilu
        nm1[rows, :] = nrm
        iv1[rows, :] = inv
        return c

    loop('mesh_embed', 0, n_mesh // BLK_M, mesh_embed, 0)

    def hots(i, c):
        rows = blk(i, 128)
        src = edge_src[pl.ds(i, 1), :]
        dst = edge_dst[pl.ds(i, 1), :]
        oh_src[rows, :] = one_hot(columns_of(src), n_grid)
        oh_dst[rows, :] = one_hot(columns_of(dst), n_mesh)
        oht_src[:, rows] = one_hot_t(src, n_grid)
        oht_dst[:, rows] = one_hot_t(dst, n_mesh)
        return c

    loop('hots', 0, n_edge // 128, hots, 0)
    stage1(0)

    def edge_embed(i, c):
        rows = blk(i, BLK_E)
        out, hid, dsilu, nrm, inv = mlp_fwd(2, mm_tn(edge_static[:, rows], w_edge_in[...]))
        lat = out.astype(BF16)
        edge_lat[rows, :] = lat
        hid2[rows, :] = hid
        ds2[rows, :] = dsilu
        nm2[rows, :] = nrm
        iv2[rows, :] = inv
        recv = mm(oh_dst[rows, :], mesh_lat[...]).astype(BF16)
        part3[rows, :] = mm(lat, w_edge_up[0:LAT, :]) + mm(recv, w_edge_up[2 * LAT:3 * LAT, :])
        return c

    loop('edge_embed', 0, n_edge // BLK_E, edge_embed, 0)
    stage2(0)

    with jax.named_scope('w_fwd'):
        for copy in fwd:
            copy.wait_recv()

    def edge_update(i, c):
        rows = blk(i, BLK_E)
        sender = mm(oh_src[rows, :], incoming[...]).astype(BF16)
        out, hid, dsilu, nrm, inv = mlp_fwd(3, part3[rows, :] + mm(sender, w_edge_up[LAT:2 * LAT, :]))
        edge_new[rows, :] = (edge_lat[rows, :].astype(F32) + out).astype(BF16)
        hid3[rows, :] = hid
        ds3[rows, :] = dsilu
        nm3[rows, :] = nrm
        iv3[rows, :] = inv
        return c

    loop('edge_update', 0, n_edge // BLK_E, edge_update, 0)
    stage3(0)

    def mesh_update(i, sums):
        rows = blk(i, BLK_M)
        total = mm(oht_dst[rows, :], edge_new[...]).astype(BF16)
        agg[rows, :] = total
        lat = mesh_lat[rows, :]
        out, hid, dsilu, nrm, inv = mlp_fwd(4, mm(lat, w_mesh_up[0:LAT, :]) + mm(total, w_mesh_up[LAT:2 * LAT, :]))
        mesh_out[rows, :] = (lat.astype(F32) + out).astype(BF16)
        d_out = d_mesh_out[rows, :].astype(F32)
        d_lin, d_pre, add = mlp_bwd(4, dsilu, nrm, inv, d_out)
        hid4[rows, :] = hid
        dl_m[rows, :] = d_lin
        dp_m[rows, :] = d_pre
        d_mesh_lat[rows, :] = d_out + mm_nt(d_pre, w_mesh_up[0:LAT, :])
        d_agg[rows, :] = mm_nt(d_pre, w_mesh_up[LAT:2 * LAT, :]).astype(BF16)
        return add4(sums, add)

    put_vec(4, loop('mesh_update', 0, n_mesh // BLK_M, mesh_update, zeros4))
    par1[0:256, :] = mm_tn(mesh_lat[...], dp_m[...])
    par1[256:512, :] = mm_tn(agg[...], dp_m[...])
    par1[512:768, :] = mm_tn(hid4[...], dl_m[...])
    stage0(1)

    def edge_back(i, sums):
        rows = blk(i, BLK_E)
        d_out = mm(oh_dst[rows, :], d_agg[...])
        d_lin, d_pre, add = mlp_bwd(3, ds3[rows, :], nm3[rows, :], iv3[rows, :], d_out)
        dl_e[rows, :] = d_lin
        dp_e[rows, :] = d_pre
        part3[rows, :] = d_out + mm_nt(d_pre, w_edge_up[0:LAT, :])
        return add4(sums, add)

    half_way = (n_edge // BLK_E + 1) // 2
    sums3 = loop('edge_back', 0, half_way, edge_back, zeros4)
    stage1(1)
    put_vec(3, loop('edge_back', half_way, n_edge // BLK_E, edge_back, sums3))

    def slot_back(i, c):
        rows = blk(i, BLK_S)
        d_sum = mm(oht_src[rows, :], dp_e[...]).astype(BF16)
        d_slot[rows, :] = d_sum
        d_incoming[rows, :] = mm_nt(d_sum, w_edge_up[LAT:2 * LAT, :]).astype(BF16)
        return c

    loop('slot_back', 0, n_grid // BLK_S, slot_back, 0)
    bwd = exchange(d_incoming, d_outgoing, b_send, b_recv)

    def node_back(i, c):
        rows = blk(i, BLK_M)
        d_sum = mm(oht_dst[rows, :], dp_e[...]).astype(BF16)
        d_node[rows, :] = d_sum
        d_mesh_lat[rows, :] = d_mesh_lat[rows, :] + mm_nt(d_sum, w_edge_up[2 * LAT:3 * LAT, :])
        return c

    loop('node_back', 0, n_mesh // BLK_M, node_back, 0)
    par2[0:256, :] = mm_tn(edge_lat[...], dp_e[...])
    par2[256:512, :] = mm_tn(incoming[...], d_slot[...])
    par2[512:768, :] = mm_tn(mesh_lat[...], d_node[...])
    par2[768:1024, :] = mm_tn(hid3[...], dl_e[...])
    stage0(2)

    def mesh_in_back(i, sums):
        rows = blk(i, BLK_M)
        d_lin, d_pre, add = mlp_bwd(1, ds1[rows, :], nm1[rows, :], iv1[rows, :], d_mesh_lat[rows, :])
        dl_m[rows, :] = d_lin
        dp_m[rows, :] = d_pre
        return add4(sums, add)

    put_vec(1, loop('mesh_in_back', 0, n_mesh // BLK_M, mesh_in_back, zeros4))
    stage1(2)

    def edge_in_back(i, sums):
        rows = blk(i, BLK_E)
        d_lin, d_pre, add = mlp_bwd(2, ds2[rows, :], nm2[rows, :], iv2[rows, :], part3[rows, :])
        dl_e[rows, :] = d_lin
        dp_e[rows, :] = d_pre
        return add4(sums, add)

    put_vec(2, loop('edge_in_back', 0, n_edge // BLK_E, edge_in_back, zeros4))
    par3[0:256, :] = mm_tn(hid2[...], dl_e[...])
    par3[256:512, :] = mm_tn(hid1[...], dl_m[...])
    stage0(3)
    stage2(1)
    par4[256 + ROW_EDGE_IN:256 + ROW_EDGE_IN + 4, :] = mm(edge_static[...], dp_e[...])
    par4[256 + ROW_MESH_IN:256 + ROW_MESH_IN + 3, :] = mm(mesh_static[...], dp_m[...])
    stage1(3)

    with jax.named_scope('w_bwd'):
        for copy in bwd:
            copy.wait_recv()

    all_rows = jnp.concatenate([row_pair(i) for i in range(N_DEV // 2)], axis=1)

    def grid_in_back(i, sums):
        rows = blk(i, BLK_G)
        sub = lax.broadcasted_iota(jnp.int32, (BLK_G, N_DEV * slots), 0) + i * BLK_G
        spread = jnp.where(sub == all_rows, 1.0, 0.0).astype(BF16)
        d_out = d_grid_lat[rows, :] + mm(spread, d_outgoing[...])
        d_lin, d_pre, add = mlp_bwd(0, ds0[rows, :], nm0[rows, :], iv0[rows, :], d_out)
        dl_g[rows, :] = d_lin
        dp_g[rows, :] = d_pre
        d_grid_in[:, rows] = mm_nt(w_grid_in[...], d_pre)
        return add4(sums, add)

    put_vec(0, loop('grid_in_back', 0, n_grid // BLK_G, grid_in_back, zeros4))
    with jax.named_scope("dw0"):
        par4[0:256, :] = mm_tn(hid0[...], dl_g[...])
        par4[256:256 + grid_in.shape[0], :] = mm(grid_in[...], dp_g[...])
        stage0(4)
    stage2(2)
    stage1(4)
    stage2(3)
    stage3(1)
    stage2(4)
    stage3(2)
    stage3(3)
    stage3(4)
    for g in range(N_GROUP):
        stage4(g)
    with jax.named_scope("t_send"):
        for copy in pending:
            copy.wait_send()


def final_kernel(mesh_res, grid_res, d_grid_res, res0, res1, res2, res3, res4,
                 mesh_out, grid_out, d_grid_in, d_w_grid_in, d_w_mesh_in, d_w_edge_in, d_w_edge_up, d_w_mesh_up, d_w_grid_up, d_w_second, d_vectors):
    mesh_out[...] = mesh_res[...]
    grid_out[...] = grid_res[...]
    d_grid_in[...] = d_grid_res[...]
    d_w_grid_up[...] = res0[0:256, :].astype(F32)
    d_w_second[5] = res0[256:512, :].astype(F32)
    d_w_mesh_up[...] = res1[0:512, :].astype(F32)
    d_w_second[4] = res1[512:768, :].astype(F32)
    d_w_edge_up[...] = res2[0:768, :].astype(F32)
    d_w_second[3] = res2[768:1024, :].astype(F32)
    d_w_second[2] = res3[0:256, :].astype(F32)
    d_w_second[1] = res3[256:512, :].astype(F32)
    d_w_second[0] = res4[0:256, :].astype(F32)
    small = res4[256:512, :].astype(F32)
    d_w_grid_in[...] = small[0:d_w_grid_in.shape[0], :]
    d_w_edge_in[...] = small[ROW_EDGE_IN:ROW_EDGE_IN + 4, :]
    d_w_mesh_in[...] = small[ROW_MESH_IN:ROW_MESH_IN + 3, :]
    d_vectors[...] = small[ROW_VEC:ROW_VEC + 24, :].reshape(6, 4, LAT)


def solution(mesh):
    row_spec = P(AXIS_NAME, None)
    edge_spec = P(AXIS_NAME)
    rep_spec = P()
    in_specs = (row_spec, row_spec, row_spec, row_spec, edge_spec, edge_spec) + (rep_spec,) * 8 + (row_spec, row_spec)
    out_specs = (row_spec, row_spec, row_spec) + (rep_spec,) * 8

    def local_step(grid_in, mesh_static, edge_static, send_rows, edge_src, edge_dst, *rest):
        n_grid, feats = grid_in.shape
        n_mesh = mesh_static.shape[0]
        n_edge = edge_static.shape[0]
        n_slot = send_rows.size
        src2 = edge_src.reshape(n_edge // 128, 128)
        dst2 = edge_dst.reshape(n_edge // 128, 128)

        def vm(shape, dtype):
            return pltpu.VMEM(shape, dtype)

        def rows_bf(n):
            return vm((n, LAT), BF16)

        def rows_f32(n):
            return vm((n, LAT), F32)

        dma = pltpu.SemaphoreType.DMA
        scratch = [
            rows_bf(n_grid), rows_bf(n_mesh), rows_bf(n_edge), rows_bf(n_slot), rows_bf(n_slot), rows_bf(n_slot), rows_bf(n_slot),
            vm((n_edge, n_slot), BF16), vm((n_slot, n_edge), BF16), vm((n_edge, n_mesh), BF16), vm((n_mesh, n_edge), BF16),
            rows_bf(n_grid), rows_bf(n_mesh), rows_bf(n_edge), rows_bf(n_edge), rows_bf(n_mesh), rows_bf(n_grid),
            rows_f32(n_grid), rows_f32(n_mesh), rows_f32(n_edge), rows_f32(n_edge),
            rows_f32(n_grid), rows_f32(n_mesh), rows_f32(n_edge), rows_f32(n_edge),
            vm((n_grid, 1), F32), vm((n_mesh, 1), F32), vm((n_edge, 1), F32), vm((n_edge, 1), F32),
            rows_f32(n_edge), rows_bf(n_edge), rows_bf(n_mesh), rows_f32(n_grid), rows_f32(n_mesh), rows_bf(n_mesh), rows_bf(n_slot), rows_bf(n_mesh),
            rows_bf(n_grid), rows_bf(n_grid), rows_bf(n_mesh), rows_bf(n_mesh), rows_bf(n_edge), rows_bf(n_edge),
        ]
        scratch += [rows_f32(r) for r in GROUP_ROWS]
        scratch += [rows_f32(r // 2) for r in GROUP_ROWS]
        scratch += [rows_bf(r // 2) for r in GROUP_ROWS]
        scratch += [vm((7, r // 16, LAT), BF16) for r in GROUP_ROWS]
        scratch += [dma((16,)), dma((16,)), dma((16,)), dma((16,)), ] + [dma((N_GROUP,)), dma((N_GROUP,)), dma((N_GROUP, 8)), dma((N_GROUP, 8)), dma((N_GROUP, 8)), dma((N_GROUP, 8)), dma((N_GROUP,)), dma((N_GROUP,))]
        shape = jax.ShapeDtypeStruct
        outs = (shape((n_mesh, LAT), BF16), shape((n_grid, LAT), BF16), shape((feats, n_grid), F32)) + tuple(shape((r, LAT), BF16) for r in GROUP_ROWS)
        vspec = pl.BlockSpec(memory_space=pltpu.VMEM)
        results = pl.pallas_call(
            main_kernel,
            out_shape=outs,
            in_specs=[vspec] * 16,
            out_specs=tuple([vspec] * len(outs)),
            scratch_shapes=scratch,
            compiler_params=pltpu.CompilerParams(collective_id=0, has_side_effects=True, vmem_limit_bytes=47 * 1024 * 1024),
        )(grid_in.T, mesh_static.T, edge_static.T, send_rows, src2, dst2, *rest)

        finals = (shape((n_mesh, LAT), BF16), shape((n_grid, LAT), BF16), shape((feats, n_grid), F32),
                  shape((feats, LAT), F32), shape((3, LAT), F32), shape((4, LAT), F32), shape((3 * LAT, LAT), F32),
                  shape((2 * LAT, LAT), F32), shape((LAT, LAT), F32), shape((6, LAT, LAT), F32), shape((6, 4, LAT), F32))
        done = pl.pallas_call(
            final_kernel,
            out_shape=finals,
            in_specs=[vspec] * len(outs),
            out_specs=tuple([vspec] * len(finals)),
            compiler_params=pltpu.CompilerParams(vmem_limit_bytes=16 * 1024 * 1024),
        )(*results)
        return done[:2] + (done[2].T,) + done[3:]

    return jax.shard_map(local_step, mesh=mesh, in_specs=in_specs, out_specs=out_specs, check_vma=False)
```

time: 79.7 us -> 69 us (0.87)
  Pallas kernels: 71.3 us -> 54.2 us
  local copies, waits for them, and re-layouts: 7.53 us -> 13.4 us
    pallas_call x1, Pallas kernels: 67 us -> 51.7 us  [local_step(): pl.pallas_call(main_kernel, out_shape=outs, in_specs=[vspec] * 16, out_sp...]
    unnamed x3 -> x32, local copies, waits for them, and re-layouts: 5.14 us -> 13.4 us
    pallas_call x1 -> x0, local copies, waits for them, and re-layouts: 2.38 us -> none  [local_step(): pl.pallas_call(final_kernel, out_shape=finals, in_specs=[vspec] * len(out...]
    pallas_call x1, Pallas kernels: 4.3 us -> 2.5 us  [local_step(): pl.pallas_call(final_kernel, out_shape=finals, in_specs=[vspec] * len(out...]
where the time goes in v2:
time: 69 us; the launch traced here: 68.3 us
  Pallas kernels  54.2 us (79%)
  local copies, waits for them, and re-layouts  13.4 us (19%)
    pallas_call x1, Pallas kernels, local_step(): pl.pallas_call(main_kernel, out_shape=outs, in_specs=[vspec] * 16, out_sp...  51.7 us
    unnamed x32, local copies, waits for them, and re-layouts  13.4 us
    pallas_call x1, Pallas kernels, local_step(): pl.pallas_call(final_kernel, out_shape=finals, in_specs=[vspec] * len(out...  2.5 us

profile of v2, /device:TPU:0, one launch (start us, length us, event | category | flops | bytes accessed | tf_op | source)
XLA Modules:
  0.0 68.3 jit_solution(1023831495916327206)
XLA Ops:
  0.7 0.0 copy-start
  0.7 1.1 %copy-done = bf16[6,256,256]{2,1,0:T(8,128)(2,1)S(1)} copy-done((bf16[6,256,256]{2,1,0:T(8,128)(2,1)S(1)}, bf16[6,256,256]{2,1,0:T(8,128)(2,1)}, u32[]{:S(2)}) %copy-start) | copy-done | bytes 786456
  1.8 0.0 copy-start.1
  1.8 1.0 %copy-done.1 = bf16[1024,256]{1,0:T(8,128)(2,1)S(1)} copy-done((bf16[1024,256]{1,0:T(8,128)(2,1)S(1)}, bf16[1024,256]{1,0:T(8,128)(2,1)}, u32[]{:S(2)}) %copy-start.1) | copy-done | bytes 524312
  2.8 0.0 copy-start.2
  2.8 1.0 %copy-done.2 = bf16[768,256]{1,0:T(8,128)(2,1)S(1)} copy-done((bf16[768,256]{1,0:T(8,128)(2,1)S(1)}, bf16[768,256]{1,0:T(8,128)(2,1)}, u32[]{:S(2)}) %copy-start.2) | copy-done | bytes 393240
  3.8 0.0 copy-start.3
  3.8 1.0 %copy-done.3 = bf16[1024,164]{0,1:T(8,128)(2,1)S(1)} copy-done((bf16[1024,164]{0,1:T(8,128)(2,1)S(1)}, bf16[1024,164]{0,1:T(8,128)(2,1)}, u32[]{:S(2)}) %copy-start.3) | copy-done | bytes 335896
  4.8 0.0 copy-start.4
  4.8 0.9 %copy-done.4 = bf16[512,256]{1,0:T(8,128)(2,1)S(1)} copy-done((bf16[512,256]{1,0:T(8,128)(2,1)S(1)}, bf16[512,256]{1,0:T(8,128)(2,1)}, u32[]{:S(2)}) %copy-start.4) | copy-done | bytes 262168
  5.8 0.0 copy-start.5
  5.8 0.9 %copy-done.5 = bf16[512,256]{1,0:T(8,128)(2,1)S(1)} copy-done((bf16[512,256]{1,0:T(8,128)(2,1)S(1)}, bf16[512,256]{1,0:T(8,128)(2,1)}, u32[]{:S(2)}) %copy-start.5) | copy-done | bytes 262168
  6.7 0.0 copy-start.6
  6.7 0.9 %copy-done.6 = bf16[256,256]{1,0:T(8,128)(2,1)S(1)} copy-done((bf16[256,256]{1,0:T(8,128)(2,1)S(1)}, bf16[256,256]{1,0:T(8,128)(2,1)}, u32[]{:S(2)}) %copy-start.6) | copy-done | bytes 131096
  7.6 0.0 copy-start.7
  7.6 0.9 %copy-done.7 = bf16[164,256]{1,0:T(8,128)(2,1)S(1)} copy-done((bf16[164,256]{1,0:T(8,128)(2,1)S(1)}, bf16[164,256]{1,0:T(8,128)(2,1)}, u32[]{:S(2)}) %copy-start.7) | copy-done | bytes 83992
  8.5 0.0 copy-start.8
  8.5 0.7 %copy-done.8 = f32[6,4,256]{2,1,0:T(4,128)S(1)} copy-done((f32[6,4,256]{2,1,0:T(4,128)S(1)}, f32[6,4,256]{2,1,0:T(4,128)}, u32[]{:S(2)}) %copy-start.8) | copy-done | bytes 24600
  9.2 0.0 copy-start.9
  9.2 0.7 %copy-done.9 = bf16[1536,4]{0,1:T(4,128)(2,1)S(1)} copy-done((bf16[1536,4]{0,1:T(4,128)(2,1)S(1)}, bf16[1536,4]{0,1:T(4,128)(2,1)}, u32[]{:S(2)}) %copy-start.9) | copy-done | bytes 12312
  9.9 0.0 copy-start.10
  9.9 0.7 %copy-done.10 = s32[16,64]{1,0:T(8,128)S(1)} copy-done((s32[16,64]{1,0:T(8,128)S(1)}, s32[16,64]{1,0:T(8,128)}, u32[]{:S(2)}) %copy-start.10) | copy-done | bytes 4120
  10.6 0.7 %copy-done.11 = s32[1536]{0:T(1024)S(1)} copy-done((s32[1536]{0:T(1024)S(1)}, s32[1536]{0:T(1024)}, u32[]{:S(2)}) %copy-start.11) | copy-done | bytes 6168
  11.3 0.0 copy-start.12
  11.3 0.7 %copy-done.12 = s32[1536]{0:T(1024)S(1)} copy-done((s32[1536]{0:T(1024)S(1)}, s32[1536]{0:T(1024)}, u32[]{:S(2)}) %copy-start.12) | copy-done | bytes 6168
  12.0 0.0 copy-start.13
  12.0 0.7 %copy-done.13 = bf16[512,3]{0,1:T(4,128)(2,1)S(1)} copy-done((bf16[512,3]{0,1:T(4,128)(2,1)S(1)}, bf16[512,3]{0,1:T(4,128)(2,1)}, u32[]{:S(2)}) %copy-start.13) | copy-done | bytes 3096
  12.7 0.0 copy-start.14
  12.7 0.7 copy-done.14
  13.4 0.7 copy-done.15
  14.1 51.7 %shard_map.239 = (bf16[512,256]{1,0:T(8,128)(2,1)S(1)}, bf16[1024,256]{1,0:T(8,128)(2,1)S(1)}, f32[164,1024]{1,0:T(8,128)S(1)}, bf16[512,256]{1,0:T(8,128)(2,1)S...) custom-call(bf16[164,1024]{1,0:T(8,128)(2,1)S(1)} %bitcast.6, ...), custom_call_target="tpu_custom_call" | custom-call | tf_op jit(solution)/shard_map/pallas_call | solution.py:491
  65.8 2.5 %shard_map.240 = (bf16[512,256]{1,0:T(8,128)(2,1)}, bf16[1024,256]{1,0:T(8,128)(2,1)}, f32[164,1024]{1,0:T(8,128)}, f32[164,256]{1,0:T(8,128)}, f32[3,256]{1,0:T...) custom-call(bf16[512,256]{1,0:T(8,128)(2,1)S(1)} %get-tuple-element., ...), custom_call_target="tpu_custom_call" | custom-call | tf_op jit(solution)/shard_map/pallas_call | solution.py:503
  (2 shorter events, 0.0 us)
Async XLA Ops:
  0.7 1.1 %copy-start = (bf16[6,256,256]{2,1,0:T(8,128)(2,1)S(1)}, bf16[6,256,256]{2,1,0:T(8,128)(2,1)}, u32[]{:S(2)}) copy-start(bf16[6,256,256]{2,1,0:T(8,128)(2,1)} %w_second.1) | copy-start | bytes 2359300
  1.8 1.0 %copy-start.1 = (bf16[1024,256]{1,0:T(8,128)(2,1)S(1)}, bf16[1024,256]{1,0:T(8,128)(2,1)}, u32[]{:S(2)}) copy-start(bf16[1024,256]{1,0:T(8,128)(2,1)} %d_grid_out.1) | copy-start | bytes 1572868
  2.8 1.0 %copy-start.2 = (bf16[768,256]{1,0:T(8,128)(2,1)S(1)}, bf16[768,256]{1,0:T(8,128)(2,1)}, u32[]{:S(2)}) copy-start(bf16[768,256]{1,0:T(8,128)(2,1)} %w_edge_up.1) | copy-start | bytes 1179652
  3.8 1.0 %copy-start.3 = (bf16[1024,164]{0,1:T(8,128)(2,1)S(1)}, bf16[1024,164]{0,1:T(8,128)(2,1)}, u32[]{:S(2)}) copy-start(bf16[1024,164]{0,1:T(8,128)(2,1)} %param.16) | copy-start | bytes 1007620
  4.8 0.9 %copy-start.4 = (bf16[512,256]{1,0:T(8,128)(2,1)S(1)}, bf16[512,256]{1,0:T(8,128)(2,1)}, u32[]{:S(2)}) copy-start(bf16[512,256]{1,0:T(8,128)(2,1)} %w_mesh_up.1) | copy-start | bytes 786436
  5.8 0.9 %copy-start.5 = (bf16[512,256]{1,0:T(8,128)(2,1)S(1)}, bf16[512,256]{1,0:T(8,128)(2,1)}, u32[]{:S(2)}) copy-start(bf16[512,256]{1,0:T(8,128)(2,1)} %d_mesh_out.1) | copy-start | bytes 786436
  6.7 0.9 %copy-start.6 = (bf16[256,256]{1,0:T(8,128)(2,1)S(1)}, bf16[256,256]{1,0:T(8,128)(2,1)}, u32[]{:S(2)}) copy-start(bf16[256,256]{1,0:T(8,128)(2,1)} %w_grid_up.1) | copy-start | bytes 393220
  7.6 0.9 %copy-start.7 = (bf16[164,256]{1,0:T(8,128)(2,1)S(1)}, bf16[164,256]{1,0:T(8,128)(2,1)}, u32[]{:S(2)}) copy-start(bf16[164,256]{1,0:T(8,128)(2,1)} %w_grid_in.1) | copy-start | bytes 251908
  8.5 0.7 %copy-start.8 = (f32[6,4,256]{2,1,0:T(4,128)S(1)}, f32[6,4,256]{2,1,0:T(4,128)}, u32[]{:S(2)}) copy-start(f32[6,4,256]{2,1,0:T(4,128)} %vectors.1) | copy-start | bytes 73732
  9.2 0.7 %copy-start.9 = (bf16[1536,4]{0,1:T(4,128)(2,1)S(1)}, bf16[1536,4]{0,1:T(4,128)(2,1)}, u32[]{:S(2)}) copy-start(bf16[1536,4]{0,1:T(4,128)(2,1)} %param.18) | copy-start | bytes 36868
  9.9 0.7 %copy-start.10 = (s32[16,64]{1,0:T(8,128)S(1)}, s32[16,64]{1,0:T(8,128)}, u32[]{:S(2)}) copy-start(s32[16,64]{1,0:T(8,128)} %send_rows.1) | copy-start | bytes 12292
  10.6 0.7 %copy-start.11 = (s32[1536]{0:T(1024)S(1)}, s32[1536]{0:T(1024)}, u32[]{:S(2)}) copy-start(s32[1536]{0:T(1024)} %param.20) | copy-start | bytes 18436
  11.3 0.7 %copy-start.12 = (s32[1536]{0:T(1024)S(1)}, s32[1536]{0:T(1024)}, u32[]{:S(2)}) copy-start(s32[1536]{0:T(1024)} %param.21) | copy-start | bytes 18436
  12.0 0.7 %copy-start.13 = (bf16[512,3]{0,1:T(4,128)(2,1)S(1)}, bf16[512,3]{0,1:T(4,128)(2,1)}, u32[]{:S(2)}) copy-start(bf16[512,3]{0,1:T(4,128)(2,1)} %param.17) | copy-start | bytes 9220
  12.7 0.7 copy-start.14
  13.4 0.7 copy-start.15

commit v3 on v2

--- a/solution.py
+++ b/solution.py
@@ -12,7 +12,7 @@
 N_DEV = 16
 N_CHIP = 8
 LAT = 256
-BLK_G, BLK_M, BLK_E, BLK_S = 1024, 512, 768, 1024
+BLK_G, BLK_M, BLK_E, BLK_S = 1024, 512, 768, 512
 F32 = jnp.float32
 BF16 = jnp.bfloat16
 
@@ -40,9 +40,10 @@
 
 
 def main_kernel(
-        grid_in, mesh_static, edge_static, send_rows, edge_src, edge_dst,
-        w_grid_in, w_mesh_in, w_edge_in, w_edge_up, w_mesh_up, w_grid_up, w_second, vectors, d_mesh_out, d_grid_out,
+        hbm_grid_in, hbm_mesh_static, hbm_edge_static, hbm_send_rows, hbm_edge_src, hbm_edge_dst,
+        hbm_w_grid_in, hbm_w_mesh_in, hbm_w_edge_in, hbm_w_edge_up, hbm_w_mesh_up, hbm_w_grid_up, hbm_w_second, hbm_vectors, hbm_d_mesh_out, hbm_d_grid_out,
         mesh_out, grid_out, d_grid_in, res0, res1, res2, res3, res4,
+        grid_in, mesh_static, edge_static, send_rows, edge_src, edge_dst, w_grid_in, w_mesh_in, w_edge_in, w_edge_up, w_mesh_up, w_grid_up, w_second, vectors, d_mesh_out, d_grid_out, in_sem,
         grid_lat, mesh_lat, edge_lat, outgoing, incoming, d_incoming, d_outgoing,
         oh_src, oht_src, oh_dst, oht_dst,
         hid0, hid1, hid2, hid3, hid4, hid5,
@@ -76,6 +77,34 @@
     for j in range(1, N_DEV):
         pl.semaphore_signal(barrier, inc=1, device_id=(flip(me, j),), device_id_type=pl.DeviceIdType.MESH)
 
+    order = ('send_rows', 'grid_in', 'w_grid_in', 'vectors', 'w_second', 'w_grid_up', 'd_grid_out', 'mesh_static', 'w_mesh_in', 'edge_src',
+             'edge_dst', 'edge_static', 'w_edge_in', 'w_edge_up', 'w_mesh_up', 'd_mesh_out')
+    loads = {
+        'grid_in': (hbm_grid_in, grid_in),
+        'mesh_static': (hbm_mesh_static, mesh_static),
+        'edge_static': (hbm_edge_static, edge_static),
+        'send_rows': (hbm_send_rows, send_rows),
+        'edge_src': (hbm_edge_src, edge_src),
+        'edge_dst': (hbm_edge_dst, edge_dst),
+        'w_grid_in': (hbm_w_grid_in, w_grid_in),
+        'w_mesh_in': (hbm_w_mesh_in, w_mesh_in),
+        'w_edge_in': (hbm_w_edge_in, w_edge_in),
+        'w_edge_up': (hbm_w_edge_up, w_edge_up),
+        'w_mesh_up': (hbm_w_mesh_up, w_mesh_up),
+        'w_grid_up': (hbm_w_grid_up, w_grid_up),
+        'w_second': (hbm_w_second, w_second),
+        'vectors': (hbm_vectors, vectors),
+        'd_mesh_out': (hbm_d_mesh_out, d_mesh_out),
+        'd_grid_out': (hbm_d_grid_out, d_grid_out),
+    }
+    for i, name in enumerate(order):
+        loads[name] = pltpu.make_async_copy(loads[name][0], loads[name][1], in_sem.at[i])
+        loads[name].start()
+
+    def need(*which):
+        for name in which:
+            loads[name].wait()
+
     pending = []
 
     def send(src, dst, send_sem, recv_sem, dev):
@@ -85,18 +114,20 @@
         pending.append(copy)
         return copy
 
-    far_first = (15, 14, 7, 6, 11, 10, 13, 12, 3, 2, 5, 4, 9, 8, 1)
+    far, near = (15, 14, 11, 10, 13, 12, 9, 8), (7, 6, 3, 2, 5, 4, 1)
+    z_bit = me // 8
     chip_order = (7, 3, 5, 6, 1, 2, 4)
 
-    def exchange(src, dst, send_sem, recv_sem):
+    def exchange(src, dst, send_sem, recv_sem, peers):
         copies = []
-        for j in far_first:
+        for j in peers:
             peer = flip(me, j)
             copies.append(send(src.at[pl.ds(pl.multiple_of(peer * slots, slots), slots)],
                                dst.at[pl.ds(pl.multiple_of(me * slots, slots), slots)],
                                send_sem.at[j], recv_sem.at[j], peer))
-        mine = pl.ds(pl.multiple_of(me * slots, slots), slots)
-        dst[mine, :] = src[mine, :]
+        if peers is near:
+            mine = pl.ds(pl.multiple_of(me * slots, slots), slots)
+            dst[mine, :] = src[mine, :]
         return copies
 
     live = {}
@@ -189,6 +220,8 @@
 
     par4[256:512, :] = jnp.zeros((256, LAT), F32)
 
+    need('grid_in', 'w_grid_in', 'vectors', 'w_second')
+
     def grid_embed(i, c):
         rows = blk(i, BLK_G)
         out, hid, dsilu, nrm, inv = mlp_fwd(0, mm_tn(grid_in[:, rows], w_grid_in[...]))
@@ -202,7 +235,7 @@
     loop('grid_embed', 0, n_grid // BLK_G, grid_embed, 0)
 
     def row_pair(i):
-        return jnp.concatenate([send_rows[2 * i:2 * i + 1, :], send_rows[2 * i + 1:2 * i + 2, :]], axis=1)
+        return jnp.concatenate([send_rows[pl.ds(2 * i, 1), :], send_rows[pl.ds(2 * i + 1, 1), :]], axis=1)
 
     def columns_of(row):
         return jnp.transpose(jnp.broadcast_to(row, (128, 128)))
@@ -216,13 +249,21 @@
         sub = lax.broadcasted_iota(jnp.int32, (n, 128), 0).astype(jnp.int16)
         return jnp.where(sub == jnp.broadcast_to(row, (n, 128)).astype(jnp.int16), jnp.ones((), BF16), jnp.zeros((), BF16))
 
-    for i in range(N_DEV // 2):
-        pick = one_hot(columns_of(row_pair(i)), n_grid)
-        outgoing[128 * i:128 * (i + 1), :] = mm(pick, grid_lat[...]).astype(BF16)
-
+    need('send_rows')
+    def gather_half(half):
+        for t in range(N_DEV // 4):
+            i = half * (N_DEV // 4) + t
+            pick = one_hot(columns_of(row_pair(i)), n_grid)
+            outgoing[blk(i, 128), :] = mm(pick, grid_lat[...]).astype(BF16)
+
+    gather_half(1 - z_bit)
     with jax.named_scope('w_bar'):
         pl.semaphore_wait(barrier, N_DEV - 1)
-    fwd = exchange(outgoing, incoming, f_send, f_recv)
+    fwd = exchange(outgoing, incoming, f_send, f_recv, far)
+    gather_half(z_bit)
+    fwd += exchange(outgoing, incoming, f_send, f_recv, near)
+
+    need('w_grid_up', 'd_grid_out')
 
     def grid_update(i, sums):
         rows = blk(i, BLK_G)
@@ -242,6 +283,8 @@
     par0[256:512, :] = mm_tn(hid5[...], dl_g[...])
     stage0(0)
 
+    need('mesh_static', 'w_mesh_in', 'edge_src', 'edge_dst', 'edge_static', 'w_edge_in', 'w_edge_up')
+
     def mesh_embed(i, c):
         rows = blk(i, BLK_M)
         out, hid, dsilu, nrm, inv = mlp_fwd(1, mm_tn(mesh_static[:, rows], w_mesh_in[...]))
@@ -281,7 +324,6 @@
         return c
 
     loop('edge_embed', 0, n_edge // BLK_E, edge_embed, 0)
-    stage2(0)
 
     with jax.named_scope('w_fwd'):
         for copy in fwd:
@@ -299,7 +341,9 @@
         return c
 
     loop('edge_update', 0, n_edge // BLK_E, edge_update, 0)
-    stage3(0)
+    stage2(0)
+
+    need('w_mesh_up', 'd_mesh_out')
 
     def mesh_update(i, sums):
         rows = blk(i, BLK_M)
@@ -332,10 +376,8 @@
         part3[rows, :] = d_out + mm_nt(d_pre, w_edge_up[0:LAT, :])
         return add4(sums, add)
 
-    half_way = (n_edge // BLK_E + 1) // 2
-    sums3 = loop('edge_back', 0, half_way, edge_back, zeros4)
+    put_vec(3, loop('edge_back', 0, n_edge // BLK_E, edge_back, zeros4))
     stage1(1)
-    put_vec(3, loop('edge_back', half_way, n_edge // BLK_E, edge_back, sums3))
 
     def slot_back(i, c):
         rows = blk(i, BLK_S)
@@ -344,8 +386,12 @@
         d_incoming[rows, :] = mm_nt(d_sum, w_edge_up[LAT:2 * LAT, :]).astype(BF16)
         return c
 
-    loop('slot_back', 0, n_grid // BLK_S, slot_back, 0)
-    bwd = exchange(d_incoming, d_outgoing, b_send, b_recv)
+    with jax.named_scope('slot_back'):
+        slot_back(1 - z_bit, 0)
+    bwd = exchange(d_incoming, d_outgoing, b_send, b_recv, far)
+    with jax.named_scope('slot_back'):
+        slot_back(z_bit, 0)
+    bwd += exchange(d_incoming, d_outgoing, b_send, b_recv, near)
 
     def node_back(i, c):
         rows = blk(i, BLK_M)
@@ -369,8 +415,6 @@
         return add4(sums, add)
 
     put_vec(1, loop('mesh_in_back', 0, n_mesh // BLK_M, mesh_in_back, zeros4))
-    stage1(2)
-
     def edge_in_back(i, sums):
         rows = blk(i, BLK_E)
         d_lin, d_pre, add = mlp_bwd(2, ds2[rows, :], nm2[rows, :], iv2[rows, :], part3[rows, :])
@@ -382,7 +426,9 @@
     par3[0:256, :] = mm_tn(hid2[...], dl_e[...])
     par3[256:512, :] = mm_tn(hid1[...], dl_m[...])
     stage0(3)
+    stage1(2)
     stage2(1)
+    stage3(0)
     par4[256 + ROW_EDGE_IN:256 + ROW_EDGE_IN + 4, :] = mm(edge_static[...], dp_e[...])
     par4[256 + ROW_MESH_IN:256 + ROW_MESH_IN + 3, :] = mm(mesh_static[...], dp_m[...])
     stage1(3)
@@ -409,8 +455,8 @@
         par4[0:256, :] = mm_tn(hid0[...], dl_g[...])
         par4[256:256 + grid_in.shape[0], :] = mm(grid_in[...], dp_g[...])
         stage0(4)
+    stage1(4)
     stage2(2)
-    stage1(4)
     stage2(3)
     stage3(1)
     stage2(4)
@@ -470,7 +516,9 @@
             return vm((n, LAT), F32)
 
         dma = pltpu.SemaphoreType.DMA
-        scratch = [
+        args = (grid_in.T, mesh_static.T, edge_static.T, send_rows, src2, dst2) + rest
+        scratch = [vm(a.shape, a.dtype) for a in args] + [dma((len(args),))]
+        scratch += [
             rows_bf(n_grid), rows_bf(n_mesh), rows_bf(n_edge), rows_bf(n_slot), rows_bf(n_slot), rows_bf(n_slot), rows_bf(n_slot),
             vm((n_edge, n_slot), BF16), vm((n_slot, n_edge), BF16), vm((n_edge, n_mesh), BF16), vm((n_mesh, n_edge), BF16),
             rows_bf(n_grid), rows_bf(n_mesh), rows_bf(n_edge), rows_bf(n_edge), rows_bf(n_mesh), rows_bf(n_grid),
@@ -490,12 +538,12 @@
         vspec = pl.BlockSpec(memory_space=pltpu.VMEM)
         results = pl.pallas_call(
             main_kernel,
-            out_shape=outs,
-            in_specs=[vspec] * 16,
+            out_shape=tuple(pltpu.VMEM(o.shape, o.dtype) for o in outs),
+            in_specs=[pl.BlockSpec(memory_space=pltpu.MemorySpace.HBM)] * 16,
             out_specs=tuple([vspec] * len(outs)),
             scratch_shapes=scratch,
-            compiler_params=pltpu.CompilerParams(collective_id=0, has_side_effects=True, vmem_limit_bytes=47 * 1024 * 1024),
-        )(grid_in.T, mesh_static.T, edge_static.T, send_rows, src2, dst2, *rest)
+            compiler_params=pltpu.CompilerParams(collective_id=0, has_side_effects=True, vmem_limit_bytes=62300 * 1024),
+        )(*args)
 
         finals = (shape((n_mesh, LAT), BF16), shape((n_grid, LAT), BF16), shape((feats, n_grid), F32),
                   shape((feats, LAT), F32), shape((3, LAT), F32), shape((4, LAT), F32), shape((3 * LAT, LAT), F32),

time: 69 us -> 54.1 us (0.78)
  local copies, waits for them, and re-layouts: 13.4 us -> 0 us
  Pallas kernels: 54.2 us -> 53.3 us
    unnamed x32 -> x0, local copies, waits for them, and re-layouts: 13.4 us -> none
    pallas_call x1, Pallas kernels: 51.7 us -> 50.8 us  [local_step(): pl.pallas_call(main_kernel, out_shape=tuple((pltpu.VMEM(o.shape, o.dtype)...]
where the time goes in v3:
time: 54.1 us; the launch traced here: 53.9 us
  Pallas kernels  53.3 us (99%)
  between operations  0.66 us (1%)
    pallas_call x1, Pallas kernels, local_step(): pl.pallas_call(main_kernel, out_shape=tuple((pltpu.VMEM(o.shape, o.dtype)...  50.8 us
    pallas_call x1, Pallas kernels, local_step(): pl.pallas_call(final_kernel, out_shape=finals, in_specs=[vspec] * len(out...  2.5 us

profile of v3, /device:TPU:0, one launch (start us, length us, event | category | flops | bytes accessed | tf_op | source)
XLA Modules:
  0.0 53.9 jit_solution(14897527268947575729)
XLA Ops:
  0.7 50.8 %shard_map.239 = (bf16[512,256]{1,0:T(8,128)(2,1)S(1)}, bf16[1024,256]{1,0:T(8,128)(2,1)S(1)}, f32[164,1024]{1,0:T(8,128)S(1)}, bf16[512,256]{1,0:T(8,128)(2,1)S...) custom-call(bf16[164,1024]{1,0:T(8,128)(2,1)} %bitcast.6, ...), custom_call_target="tpu_custom_call" | custom-call | tf_op jit(solution)/shard_map/pallas_call | solution.py:539
  51.4 2.5 %shard_map.240 = (bf16[512,256]{1,0:T(8,128)(2,1)}, bf16[1024,256]{1,0:T(8,128)(2,1)}, f32[164,1024]{1,0:T(8,128)}, f32[164,256]{1,0:T(8,128)}, f32[3,256]{1,0:T...) custom-call(bf16[512,256]{1,0:T(8,128)(2,1)S(1)} %get-tuple-element., ...), custom_call_target="tpu_custom_call" | custom-call | tf_op jit(solution)/shard_map/pallas_call | solution.py:551

commit v4 on v3

--- a/solution.py
+++ b/solution.py
@@ -111,75 +111,70 @@
         copy = pltpu.make_async_remote_copy(src_ref=src, dst_ref=dst, send_sem=send_sem, recv_sem=recv_sem,
                                             device_id=(dev,), device_id_type=pl.DeviceIdType.MESH)
         copy.start()
-        pending.append(copy)
-        return copy
+
+    def settle(ref, sem):
+        pltpu.make_async_copy(ref, ref, sem).wait()
 
     far, near = (15, 14, 11, 10, 13, 12, 9, 8), (7, 6, 3, 2, 5, 4, 1)
     z_bit = me // 8
     chip_order = (7, 3, 5, 6, 1, 2, 4)
 
     def exchange(src, dst, send_sem, recv_sem, peers):
-        copies = []
         for j in peers:
             peer = flip(me, j)
-            copies.append(send(src.at[pl.ds(pl.multiple_of(peer * slots, slots), slots)],
-                               dst.at[pl.ds(pl.multiple_of(me * slots, slots), slots)],
-                               send_sem.at[j], recv_sem.at[j], peer))
+            send(src.at[pl.ds(pl.multiple_of(peer * slots, slots), slots)],
+                 dst.at[pl.ds(pl.multiple_of(me * slots, slots), slots)], send_sem, recv_sem, peer)
         if peers is near:
             mine = pl.ds(pl.multiple_of(me * slots, slots), slots)
             dst[mine, :] = src[mine, :]
-        return copies
-
-    live = {}
+            pending.append((src.at[pl.ds(0, (N_DEV - 1) * slots)], send_sem))
 
     def stage0(g):
         half = GROUP_ROWS[g] // 2
         other = pl.ds(pl.multiple_of((1 - core) * half, half), half)
-        live[g] = [send(pars[g].at[other], ras[g], s0_send.at[g], s0_recv.at[g], flip(me, 1))]
+        send(pars[g].at[other], ras[g], s0_send.at[g], s0_recv.at[g], flip(me, 1))
+        pending.append((ras[g], s0_send.at[g]))
 
     def stage1(g):
         with jax.named_scope('s1_%d' % g):
-            live[g][0].wait_recv()
+            settle(ras[g], s0_recv.at[g])
             half = GROUP_ROWS[g] // 2
             part = half // N_CHIP
             mine = pl.ds(pl.multiple_of(core * half, half), half)
             total = pars[g][mine, :] + ras[g][...]
             ras[g][...] = total
             css[g][...] = total.astype(BF16)
-            copies = []
             for j in chip_order:
                 peer = flip(me, 2 * j)
-                copies.append(send(css[g].at[pl.ds(pl.multiple_of((peer // 2) * part, part), part)], rbs[g].at[j - 1],
-                                   s1_send.at[g, j], s1_recv.at[g, j], peer))
-            live[g] = copies
+                send(css[g].at[pl.ds(pl.multiple_of((peer // 2) * part, part), part)], rbs[g].at[j - 1],
+                     s1_send.at[g], s1_recv.at[g], peer)
+            pending.append((rbs[g], s1_send.at[g]))
 
     def stage2(g):
         with jax.named_scope('s2_%d' % g):
             half = GROUP_ROWS[g] // 2
             part = half // N_CHIP
-            for copy in live[g]:
-                copy.wait_recv()
+            settle(rbs[g], s1_recv.at[g])
             total = ras[g][pl.ds(pl.multiple_of(chip * part, part), part), :]
             for j in range(1, N_CHIP):
                 total = total + rbs[g][j - 1].astype(F32)
             mine = pl.ds(pl.multiple_of(core * half + chip * part, part), part)
             ress[g][mine, :] = total.astype(BF16)
-            copies = []
             for j in chip_order:
-                copies.append(send(ress[g].at[mine], ress[g].at[mine], s2_send.at[g, j], s2_recv.at[g, j], flip(me, 2 * j)))
-            live[g] = copies
+                send(ress[g].at[mine], ress[g].at[mine], s2_send.at[g], s2_recv.at[g], flip(me, 2 * j))
+            pending.append((rbs[g], s2_send.at[g]))
 
     def stage3(g):
         with jax.named_scope('s3_%d' % g):
             half = GROUP_ROWS[g] // 2
-            for copy in live[g]:
-                copy.wait_recv()
+            settle(rbs[g], s2_recv.at[g])
             mine = pl.ds(pl.multiple_of(core * half, half), half)
-            live[g] = [send(ress[g].at[mine], ress[g].at[mine], s3_send.at[g], s3_recv.at[g], flip(me, 1))]
+            send(ress[g].at[mine], ress[g].at[mine], s3_send.at[g], s3_recv.at[g], flip(me, 1))
+            pending.append((css[g], s3_send.at[g]))
 
     def stage4(g):
         with jax.named_scope('s4_%d' % g):
-            live[g][0].wait_recv()
+            settle(css[g], s3_recv.at[g])
 
     def blk(i, size):
         return pl.ds(pl.multiple_of(i * size, size), size)
@@ -259,9 +254,9 @@
     gather_half(1 - z_bit)
     with jax.named_scope('w_bar'):
         pl.semaphore_wait(barrier, N_DEV - 1)
-    fwd = exchange(outgoing, incoming, f_send, f_recv, far)
+    exchange(outgoing, incoming, f_send, f_recv, far)
     gather_half(z_bit)
-    fwd += exchange(outgoing, incoming, f_send, f_recv, near)
+    exchange(outgoing, incoming, f_send, f_recv, near)
 
     need('w_grid_up', 'd_grid_out')
 
@@ -326,8 +321,7 @@
     loop('edge_embed', 0, n_edge // BLK_E, edge_embed, 0)
 
     with jax.named_scope('w_fwd'):
-        for copy in fwd:
-            copy.wait_recv()
+        settle(incoming.at[pl.ds(0, (N_DEV - 1) * slots)], f_recv)
 
     def edge_update(i, c):
         rows = blk(i, BLK_E)
@@ -388,10 +382,10 @@
 
     with jax.named_scope('slot_back'):
         slot_back(1 - z_bit, 0)
-    bwd = exchange(d_incoming, d_outgoing, b_send, b_recv, far)
+    exchange(d_incoming, d_outgoing, b_send, b_recv, far)
     with jax.named_scope('slot_back'):
         slot_back(z_bit, 0)
-    bwd += exchange(d_incoming, d_outgoing, b_send, b_recv, near)
+    exchange(d_incoming, d_outgoing, b_send, b_recv, near)
 
     def node_back(i, c):
         rows = blk(i, BLK_M)
@@ -434,8 +428,7 @@
     stage1(3)
 
     with jax.named_scope('w_bwd'):
-        for copy in bwd:
-            copy.wait_recv()
+        settle(d_outgoing.at[pl.ds(0, (N_DEV - 1) * slots)], b_recv)
 
     all_rows = jnp.concatenate([row_pair(i) for i in range(N_DEV // 2)], axis=1)
 
@@ -466,29 +459,51 @@
     for g in range(N_GROUP):
         stage4(g)
     with jax.named_scope("t_send"):
-        for copy in pending:
-            copy.wait_send()
+        for ref, sem in pending:
+            settle(ref, sem)
 
 
 def final_kernel(mesh_res, grid_res, d_grid_res, res0, res1, res2, res3, res4,
-                 mesh_out, grid_out, d_grid_in, d_w_grid_in, d_w_mesh_in, d_w_edge_in, d_w_edge_up, d_w_mesh_up, d_w_grid_up, d_w_second, d_vectors):
-    mesh_out[...] = mesh_res[...]
-    grid_out[...] = grid_res[...]
-    d_grid_in[...] = d_grid_res[...]
-    d_w_grid_up[...] = res0[0:256, :].astype(F32)
-    d_w_second[5] = res0[256:512, :].astype(F32)
-    d_w_mesh_up[...] = res1[0:512, :].astype(F32)
-    d_w_second[4] = res1[512:768, :].astype(F32)
-    d_w_edge_up[...] = res2[0:768, :].astype(F32)
-    d_w_second[3] = res2[768:1024, :].astype(F32)
-    d_w_second[2] = res3[0:256, :].astype(F32)
-    d_w_second[1] = res3[256:512, :].astype(F32)
-    d_w_second[0] = res4[0:256, :].astype(F32)
+                 mesh_out, grid_out, d_grid_in, d_w_grid_in, d_w_mesh_in, d_w_edge_in, d_w_edge_up, d_w_mesh_up, d_w_grid_up, d_w_second, d_vectors,
+                 b_grid_in, b_mesh_in, b_edge_in, b_edge_up, b_mesh_up, b_grid_up, b_second, b_vectors, sems):
+    plan = []
+    started = []
+
+    def start(src, dst):
+        copy = pltpu.make_async_copy(src, dst, sems.at[len(started)])
+        copy.start()
+        started.append(copy)
+
+    def put(src, rows, buf, dst):
+        buf[...] = src[rows[0]:rows[1], :].astype(F32)
+        plan.append((buf, dst))
+        if len(plan) > 1:
+            start(*plan[-2])
+
+    start(d_grid_res, d_grid_in)
+    start(grid_res, grid_out)
+    start(mesh_res, mesh_out)
+    put(res2, (0, 768), b_edge_up, d_w_edge_up)
+    put(res1, (0, 512), b_mesh_up, d_w_mesh_up)
+    put(res0, (0, 256), b_grid_up, d_w_grid_up)
+    put(res0, (256, 512), b_second.at[5], d_w_second.at[5])
+    put(res1, (512, 768), b_second.at[4], d_w_second.at[4])
+    put(res2, (768, 1024), b_second.at[3], d_w_second.at[3])
+    put(res3, (0, 256), b_second.at[2], d_w_second.at[2])
+    put(res3, (256, 512), b_second.at[1], d_w_second.at[1])
+    put(res4, (0, 256), b_second.at[0], d_w_second.at[0])
     small = res4[256:512, :].astype(F32)
-    d_w_grid_in[...] = small[0:d_w_grid_in.shape[0], :]
-    d_w_edge_in[...] = small[ROW_EDGE_IN:ROW_EDGE_IN + 4, :]
-    d_w_mesh_in[...] = small[ROW_MESH_IN:ROW_MESH_IN + 3, :]
-    d_vectors[...] = small[ROW_VEC:ROW_VEC + 24, :].reshape(6, 4, LAT)
+    b_edge_in[...] = small[ROW_EDGE_IN:ROW_EDGE_IN + 4, :]
+    b_mesh_in[...] = small[ROW_MESH_IN:ROW_MESH_IN + 3, :]
+    b_vectors[...] = small[ROW_VEC:ROW_VEC + 24, :].reshape(6, 4, LAT)
+    b_grid_in[...] = small[0:b_grid_in.shape[0], :]
+    start(*plan[-1])
+    start(b_edge_in, d_w_edge_in)
+    start(b_mesh_in, d_w_mesh_in)
+    start(b_vectors, d_vectors)
+    start(b_grid_in, d_w_grid_in)
+    for copy in started:
+        copy.wait()
 
 
 def solution(mesh):
@@ -532,7 +547,7 @@
         scratch += [rows_f32(r // 2) for r in GROUP_ROWS]
         scratch += [rows_bf(r // 2) for r in GROUP_ROWS]
         scratch += [vm((7, r // 16, LAT), BF16) for r in GROUP_ROWS]
-        scratch += [dma((16,)), dma((16,)), dma((16,)), dma((16,)), ] + [dma((N_GROUP,)), dma((N_GROUP,)), dma((N_GROUP, 8)), dma((N_GROUP, 8)), dma((N_GROUP, 8)), dma((N_GROUP, 8)), dma((N_GROUP,)), dma((N_GROUP,))]
+        scratch += [dma] * 4 + [dma((N_GROUP,))] * 8
         shape = jax.ShapeDtypeStruct
         outs = (shape((n_mesh, LAT), BF16), shape((n_grid, LAT), BF16), shape((feats, n_grid), F32)) + tuple(shape((r, LAT), BF16) for r in GROUP_ROWS)
         vspec = pl.BlockSpec(memory_space=pltpu.VMEM)
@@ -552,7 +567,8 @@
             final_kernel,
             out_shape=finals,
             in_specs=[vspec] * len(outs),
-            out_specs=tuple([vspec] * len(finals)),
+            out_specs=tuple([pl.BlockSpec(memory_space=pltpu.MemorySpace.HBM)] * len(finals)),
+            scratch_shapes=[vm(f.shape, f.dtype) for f in finals[3:]] + [dma((16,))],
             compiler_params=pltpu.CompilerParams(vmem_limit_bytes=16 * 1024 * 1024),
         )(*results)
         return done[:2] + (done[2].T,) + done[3:]

time: 54.1 us -> 52.2 us (0.965)
  Pallas kernels: 53.3 us -> 51.2 us
    pallas_call x1, Pallas kernels: 50.8 us -> 48.9 us  [local_step(): pl.pallas_call(main_kernel, out_shape=tuple((pltpu.VMEM(o.shape, o.dtype)...]
where the time goes in v4:
time: 52.2 us; the launch traced here: 52.1 us
  Pallas kernels  51.2 us (98%)
  between operations  0.82 us (2%)
    pallas_call x1, Pallas kernels, local_step(): pl.pallas_call(main_kernel, out_shape=tuple((pltpu.VMEM(o.shape, o.dtype)...  48.9 us
    pallas_call x1, Pallas kernels, local_step(): pl.pallas_call(final_kernel, out_shape=finals, in_specs=[vspec] * len(out...  2.35 us

profile of v4, /device:TPU:0, one launch (start us, length us, event | category | flops | bytes accessed | tf_op | source)
XLA Modules:
  0.0 52.1 jit_solution(10140843235229493576)
XLA Ops:
  0.7 48.9 %shard_map.239 = (bf16[512,256]{1,0:T(8,128)(2,1)S(1)}, bf16[1024,256]{1,0:T(8,128)(2,1)S(1)}, f32[164,1024]{1,0:T(8,128)S(1)}, bf16[512,256]{1,0:T(8,128)(2,1)S...) custom-call(bf16[164,1024]{1,0:T(8,128)(2,1)} %bitcast.6, ...), custom_call_target="tpu_custom_call" | custom-call | tf_op jit(solution)/shard_map/pallas_call | solution.py:554
  49.5 2.3 %shard_map.240 = (bf16[512,256]{1,0:T(8,128)(2,1)}, bf16[1024,256]{1,0:T(8,128)(2,1)}, f32[164,1024]{1,0:T(8,128)}, f32[164,256]{1,0:T(8,128)}, f32[3,256]{1,0:T...) custom-call(bf16[512,256]{1,0:T(8,128)(2,1)S(1)} %get-tuple-element., ...), custom_call_target="tpu_custom_call" | custom-call | tf_op jit(solution)/shard_map/pallas_call | solution.py:566

commit v5 on v4

--- a/solution.py
+++ b/solution.py
@@ -18,6 +18,7 @@
 
 GROUP_ROWS = (512, 768, 1024, 512, 512)
 N_GROUP = len(GROUP_ROWS)
+RELAYED = (1, 2, 3)
 ROW_EDGE_IN = 168
 ROW_MESH_IN = 176
 ROW_VEC = 184
@@ -51,7 +52,7 @@
         part3, edge_new, agg, d_grid_lat, d_mesh_lat, d_agg, d_slot, d_node,
         dl_g, dp_g, dl_m, dp_m, dl_e, dp_e,
         par0, par1, par2, par3, par4, ra0, ra1, ra2, ra3, ra4, cs0, cs1, cs2, cs3, cs4, rb0, rb1, rb2, rb3, rb4,
-        f_send, f_recv, b_send, b_recv, s0_send, s0_recv, s1_send, s1_recv, s2_send, s2_recv, s3_send, s3_recv):
+        f_send, f_recv, b_send, b_recv, s0_send, s0_recv, s1_send, s1_recv, s2_send, s2_recv, s3_send, s3_recv, s4_send, s4_recv):
     me = lax.axis_index(AXIS_NAME)
     core = me % 2
     chip = me // 2
@@ -160,14 +161,28 @@
                 total = total + rbs[g][j - 1].astype(F32)
             mine = pl.ds(pl.multiple_of(core * half + chip * part, part), part)
             ress[g][mine, :] = total.astype(BF16)
-            for j in chip_order:
+            peers = (7, 1, 2, 4) if g in RELAYED else chip_order
+            for j in peers:
                 send(ress[g].at[mine], ress[g].at[mine], s2_send.at[g], s2_recv.at[g], flip(me, 2 * j))
-            pending.append((rbs[g], s2_send.at[g]))
+            pending.append((rbs[g].at[pl.ds(0, len(peers))], s2_send.at[g]))
+
+    def relay(g):
+        with jax.named_scope('re_%d' % g):
+            half = GROUP_ROWS[g] // 2
+            part = half // N_CHIP
+            settle(rbs[g].at[pl.ds(0, 4)], s2_recv.at[g])
+            for origin, target in ((2, 1), (4, 2), (1, 4)):
+                rows = pl.ds(pl.multiple_of(core * half + (flip(me, 2 * origin) // 2) * part, part), part)
+                send(ress[g].at[rows], ress[g].at[rows], s4_send.at[g], s4_recv.at[g], flip(me, 2 * target))
+            pending.append((rbs[g].at[pl.ds(0, 3)], s4_send.at[g]))
 
     def stage3(g):
         with jax.named_scope('s3_%d' % g):
             half = GROUP_ROWS[g] // 2
-            settle(rbs[g], s2_recv.at[g])
+            if g in RELAYED:
+                settle(rbs[g].at[pl.ds(0, 3)], s4_recv.at[g])
+            else:
+                settle(rbs[g], s2_recv.at[g])
             mine = pl.ds(pl.multiple_of(core * half, half), half)
             send(ress[g].at[mine], ress[g].at[mine], s3_send.at[g], s3_recv.at[g], flip(me, 1))
             pending.append((css[g], s3_send.at[g]))
@@ -448,11 +463,14 @@
         par4[0:256, :] = mm_tn(hid0[...], dl_g[...])
         par4[256:256 + grid_in.shape[0], :] = mm(grid_in[...], dp_g[...])
         stage0(4)
+    relay(1)
     stage1(4)
     stage2(2)
     stage2(3)
     stage3(1)
+    relay(2)
     stage2(4)
+    relay(3)
     stage3(2)
     stage3(3)
     stage3(4)
@@ -547,7 +565,7 @@
         scratch += [rows_f32(r // 2) for r in GROUP_ROWS]
         scratch += [rows_bf(r // 2) for r in GROUP_ROWS]
         scratch += [vm((7, r // 16, LAT), BF16) for r in GROUP_ROWS]
-        scratch += [dma] * 4 + [dma((N_GROUP,))] * 8
+        scratch += [dma] * 4 + [dma((N_GROUP,))] * 10
         shape = jax.ShapeDtypeStruct
         outs = (shape((n_mesh, LAT), BF16), shape((n_grid, LAT), BF16), shape((feats, n_grid), F32)) + tuple(shape((r, LAT), BF16) for r in GROUP_ROWS)
         vspec = pl.BlockSpec(memory_space=pltpu.VMEM)

time: 52.2 us -> 52.2 us (level)
  no operation moved by 1% of the time
where the time goes in v5:
time: 52.2 us; the launch traced here: 52.1 us
  Pallas kernels  51.3 us (98%)
  between operations  0.82 us (2%)
    pallas_call x1, Pallas kernels, local_step(): pl.pallas_call(main_kernel, out_shape=tuple((pltpu.VMEM(o.shape, o.dtype)...  48.9 us
    pallas_call x1, Pallas kernels, local_step(): pl.pallas_call(final_kernel, out_shape=finals, in_specs=[vspec] * len(out...  2.35 us

profile of v5, /device:TPU:0, one launch (start us, length us, event | category | flops | bytes accessed | tf_op | source)
XLA Modules:
  0.0 52.1 jit_solution(18414553538782108358)
XLA Ops:
  0.7 48.9 %shard_map.239 = (bf16[512,256]{1,0:T(8,128)(2,1)S(1)}, bf16[1024,256]{1,0:T(8,128)(2,1)S(1)}, f32[164,1024]{1,0:T(8,128)S(1)}, bf16[512,256]{1,0:T(8,128)(2,1)S...) custom-call(bf16[164,1024]{1,0:T(8,128)(2,1)} %bitcast.6, ...), custom_call_target="tpu_custom_call" | custom-call | tf_op jit(solution)/shard_map/pallas_call | solution.py:572
  49.6 2.3 %shard_map.240 = (bf16[512,256]{1,0:T(8,128)(2,1)}, bf16[1024,256]{1,0:T(8,128)(2,1)}, f32[164,1024]{1,0:T(8,128)}, f32[164,256]{1,0:T(8,128)}, f32[3,256]{1,0:T...) custom-call(bf16[512,256]{1,0:T(8,128)(2,1)S(1)} %get-tuple-element., ...), custom_call_target="tpu_custom_call" | custom-call | tf_op jit(solution)/shard_map/pallas_call | solution.py:584
